TPU v7x, 512 devices: a whole 4x8x8 slice. The times are simulated.
512 devices in a mesh: grp: 128 (over y, z, core), slab: 4 (over x).
Axes of the slice: x: 4, y: 8, z: 8, core: 2. Of those that a mesh axis runs over, the one named last changes fastest.
Arguments:
- grids: float32 [128, 512, 4096], P('grp', 'slab'), may hold values from -6 to 6
- first_level: int32 [128], P('grp'), may hold values from 6 to 8, as said below
- coeffs: int32 [128], P('grp'), may hold values from -3 to 3
- slot_map: int32 [128, 512], P('grp', 'slab'), may hold values from 0 to 1023, as said below
Outputs:
- combined_grid: float32 [128, 512, 4096], P('grp', 'slab')
Inputs may be any that keep to these rules, and one draw needn't show every extreme that they name: The second dimension of grid g has level 9 minus first_level[g]. Every value of the range is taken by some grid. `slot_map`: grid g's point with first coordinate i of 2^a points lies at position i / 2^a of a periodic unit interval, and likewise in the second dimension. Two rows of any grids at the same position in the first two dimensions share a slot; rows of one grid have distinct slots; every slot is used by some grid. The rows held by the s-th index of slab (first coordinates in the s-th of 4 equal ranges) of every grid have slots in the s-th of 4 equal aligned ranges of the 1024 slots.
All inputs are finite; a program needn't handle non-finite values.
Results may differ from a plain program's by a relative error of at most 0.0003.
Values sent between devices are 32-bit elements; how exact they have to be, the bound alone decides.
No kernel may reach another device: no remote copies, remote signals or barrier semaphores. Data moves between devices by JAX's collectives and lax.ppermute only.
A program may use at most 64 MiB of HBM per device.

v0:
```python
import jax
import jax.numpy as jnp
from jax import lax
from jax.sharding import PartitionSpec as P

P2 = 16
P3 = 16
P4 = 16
LEVEL_SUM = 9
PLANE = 8
ROWS = 512


def joined_along(pieces, dim):
    pieces = jnp.moveaxis(pieces, 0, dim)
    shape = pieces.shape
    return pieces.reshape(*shape[:dim], shape[dim] * shape[dim + 1], *shape[dim + 2 :])


def from_everyone(x, axis):
    length = lax.axis_size(axis)
    return lax.all_to_all(jnp.broadcast_to(x[None], (length, *x.shape)), axis, 0, 0, tiled=True)


def gathered_copies(x, axis, dim):
    return joined_along(from_everyone(x, axis), dim)


def hier_weight(target, source, period):
    spread = target & -target
    interior = (target != 0).astype(jnp.float32)
    left_side = (source == target - spread).astype(jnp.float32)
    right_side = (source == (target + spread) % period).astype(jnp.float32)
    return (target == source).astype(jnp.float32) - 0.5 * interior * (left_side + right_side)


def dehier_weight(target, source, period):
    spread = jnp.maximum(source & -source, 1).astype(jnp.float32)
    apart = jnp.abs(target - source)
    apart = jnp.minimum(apart, period - apart).astype(jnp.float32)
    return jnp.where(source == 0, 1.0, jnp.maximum(0.0, 1.0 - apart / spread))


def square_table(maker, length):
    points = jnp.arange(length, dtype=jnp.int32)
    return maker(points[:, None], points[None, :], length)


def inner_apply(values, third_op, rest_op):
    count = values.shape[0]
    shaped = values.reshape(count, P2, P3 * P4)
    shaped = jnp.einsum("ij,rjk->rik", third_op, shaped, precision=lax.Precision.HIGHEST)
    shaped = jnp.einsum("rjk,lk->rjl", shaped, rest_op, precision=lax.Precision.HIGHEST)
    return shaped.reshape(count, P2 * P3 * P4)


def exact_dot(left, right):
    return jnp.dot(left, right, precision=lax.Precision.HIGHEST, preferred_element_type=jnp.float32)


def shards(grids, first_level, coeffs, slot_map):
    grid_rows = grids[0]
    level = first_level[0]
    second = LEVEL_SUM - level
    rows_dev = grid_rows.shape[0]
    width = grid_rows.shape[1]
    slabs = lax.axis_size("slab")
    slab_index = lax.axis_index("slab")
    span = rows_dev >> second
    row_ids = jnp.arange(rows_dev, dtype=jnp.int32)
    first_pos = row_ids >> second
    second_pos = row_ids & (1 << second) - 1
    slab_ids = jnp.arange(slabs, dtype=jnp.int32)
    same_first = (first_pos[:, None] == first_pos[None, :]).astype(jnp.float32)
    hier_third = square_table(hier_weight, P2)
    hier_rest = jnp.kron(square_table(hier_weight, P3), square_table(hier_weight, P4))
    values = inner_apply(grid_rows, hier_third, hier_rest)
    second_op = same_first * hier_weight(second_pos[:, None], second_pos[None, :], 1 << second)
    values = exact_dot(second_op, values)
    plane = values[:PLANE]
    planes = gathered_copies(plane[None], "slab", 0)
    following = lax.dynamic_index_in_dim(planes, (slab_index + 1) % slabs, 0, keepdims=False)
    extended = jnp.concatenate([values, following], axis=0)
    ext_ids = jnp.arange(rows_dev + PLANE, dtype=jnp.int32)
    ext_first = ext_ids >> second
    ext_second = ext_ids & (1 << second) - 1
    spread = first_pos & -first_pos
    interior = (first_pos != 0).astype(jnp.float32)[:, None]
    same_second = (second_pos[:, None] == ext_second[None, :]).astype(jnp.float32)
    centre = (ext_first[None, :] == first_pos[:, None]).astype(jnp.float32)
    below = (ext_first[None, :] == (first_pos - spread)[:, None]).astype(jnp.float32)
    above = (ext_first[None, :] == (first_pos + spread)[:, None]).astype(jnp.float32)
    fine_op = same_second * (centre - 0.5 * interior * (below + above))
    surplus = exact_dot(fine_op, extended)
    coarse_weights = hier_weight(slab_index, slab_ids, slabs)
    coarse = jnp.einsum("q,qpk->pk", coarse_weights, planes, precision=lax.Precision.HIGHEST)
    padded = jnp.concatenate([coarse, jnp.zeros((rows_dev - PLANE, width), jnp.float32)], axis=0)
    surplus = jnp.where((first_pos == 0)[:, None], padded, surplus)
    scaled = coeffs[0].astype(jnp.float32) * surplus
    per_slab = 2 * ROWS // slabs
    slot_local = slot_map[0] % per_slab
    slot_ids = jnp.arange(per_slab, dtype=jnp.int32)
    gather_op = (slot_local[None, :] == slot_ids[:, None]).astype(jnp.float32)
    term = exact_dot(gather_op, scaled)
    total = lax.psum(term, "grp")
    spread_op = (slot_local[:, None] == slot_ids[None, :]).astype(jnp.float32)
    combined = exact_dot(spread_op, total)
    back_third = square_table(dehier_weight, P2)
    back_rest = jnp.kron(square_table(dehier_weight, P3), square_table(dehier_weight, P4))
    values = inner_apply(combined, back_third, back_rest)
    back_second = same_first * dehier_weight(second_pos[:, None], second_pos[None, :], 1 << second)
    values = exact_dot(back_second, values)
    top_plane = values[:PLANE]
    top_planes = gathered_copies(top_plane[None], "slab", 0)
    here_weights = dehier_weight(slab_index, slab_ids, slabs)
    there_weights = dehier_weight((slab_index + 1) % slabs, slab_ids, slabs)
    here = jnp.einsum("q,qpk->pk", here_weights, top_planes, precision=lax.Precision.HIGHEST)
    there = jnp.einsum("q,qpk->pk", there_weights, top_planes, precision=lax.Precision.HIGHEST)
    same_row_second = (second_pos[:, None] == second_pos[None, :]).astype(jnp.float32)
    inside = (first_pos[None, :] != 0).astype(jnp.float32)
    local_op = (
        same_row_second * inside * dehier_weight(first_pos[:, None], first_pos[None, :], 2 * span)
    )
    fraction = first_pos.astype(jnp.float32) / span.astype(jnp.float32)
    plane_ids = jnp.arange(PLANE, dtype=jnp.int32)
    plane_pick = (second_pos[:, None] == plane_ids[None, :]).astype(jnp.float32)
    nodal = exact_dot(local_op, values)
    nodal = nodal + exact_dot((1.0 - fraction)[:, None] * plane_pick, here)
    nodal = nodal + exact_dot(fraction[:, None] * plane_pick, there)
    return nodal[None]


def solution(mesh):
    in_specs = (P("grp", "slab", None), P("grp"), P("grp"), P("grp", "slab"))
    out_specs = P("grp", "slab", None)
    return jax.shard_map(shards, mesh=mesh, in_specs=in_specs, out_specs=out_specs, check_vma=False)
```

profile of v0, /device:TPU:1, one launch (start us, length us, event | category | flops | bytes accessed | tf_op | source)
XLA Modules:
  0.0 292.8 jit_solution(5647194304869561142)
XLA Ops:
  7.4 2.3 copy.16
  9.7 1.9 fusion.114
  11.7 1.5 broadcast_multiply_fusion.1
  13.2 2.4 reshape.462
  15.6 3.2 %fusion.7 = f32[128,16,256]{0,2,1:T(8,128)S(1)} fusion(f32[256,256,1]{1,0,2:T(8,128)S(1)} %reshape.462, f32[16,128,256]{2,0,1:T(8,128)S(1)} %fusion.114), kind=kOutput, calls=%fused_computation.10 | convolution fusion | flops 1610612736 | bytes 4456448 | tf_op jit(solution)/shard_map/rjk,lk->rjl/dot_general | solution.py:53
  18.9 2.0 fusion.39
  21.7 4.8 %all-to-all-start = ((f32[4,1,8,4096]{3,2,1,0:T(8,128)}), f32[4,1,8,4096]{3,2,1,0:T(8,128)S(1)}, u32[]{:S(2)}, u32[]{:S(2)}) async-start(f32[4,1,8,4096]{3,2,1,0:T(8,128)} %broadcast_in_dim.69), calls=%async_computation | async-start | bytes 1048576 | tf_op jit(solution)/shard_map/all_to_all | solution.py:22
  27.3 6.2 %all-to-all-done = f32[4,1,8,4096]{3,2,1,0:T(8,128)S(1)} async-done(((f32[4,1,8,4096]{3,2,1,0:T(8,128)}), f32[4,1,8,4096]{3,2,1,0:T(8,128)S(1)}, u32[]{:S(2)}, u32[]{:S(2)}) %all-to-all-start) | async-done | bytes 524320 | tf_op jit(solution)/shard_map/all_to_all | solution.py:22
  33.5 1.2 fusion.11
  34.8 2.1 fusion.1
  36.9 3.8 %fusion.29 = f32[256,4096]{1,0:T(8,128)} fusion(f32[128,4096]{1,0:T(8,128)S(1)} %fusion.1, s32[128]{0:T(128)S(1)} %fusion.130), kind=kOutput, calls=%fused_computation.38 | convolution fusion | flops 1610645504 | bytes 6291968 | tf_op jit(solution)/shard_map/dot_general | solution.py:58
  41.1 0.9 reshape.466
  42.1 210.4 %all-reduce.3.cloned.1.call-done = f32[256,4096]{1,0:T(8,128)} async-done(((f32[256,4096]{1,0:T(8,128)}), f32[256,4096]{1,0:T(8,128)}) %all-reduce.3.cloned.1.call-update) | async-done | bytes 4194320 | tf_op jit(solution)/shard_map/psum | solution.py:105
  252.4 3.9 %fusion.28 = f32[128,4096]{1,0:T(8,128)S(1)} fusion(f32[256,4096]{1,0:T(8,128)} %all-reduce.3.cloned.1.call-done, s32[128]{0:T(128)S(1)} %and_select_fusion.3), kind=kOutput, calls=%fused_computation.37 | convolution fusion | flops 1610645504 | bytes 6291968 | tf_op jit(solution)/shard_map/dot_general | solution.py:58
  257.0 1.9 fusion.112
  258.9 3.4 %fusion.5 = f32[128,16,256]{0,2,1:T(8,128)S(1)} fusion(f32[256,256,1]{1,0,2:T(8,128)S(1)} %reshape.466, f32[128,256,16]{1,2,0:T(8,128)S(1)} %fusion.112), kind=kOutput, calls=%fused_computation.8 | convolution fusion | flops 1610612736 | bytes 4456448 | tf_op jit(solution)/shard_map/rjk,lk->rjl/dot_general | solution.py:53
  262.4 2.0 fusion.38
  265.2 4.0 %all-to-all-start.1 = ((f32[4,1,8,4096]{3,2,1,0:T(8,128)}), f32[4,1,8,4096]{3,2,1,0:T(8,128)S(1)}, u32[]{:S(2)}, u32[]{:S(2)}) async-start(f32[4,1,8,4096]{3,2,1,0:T(8,128)} %broadcast_in_dim.73), calls=%async_computation.1 | async-start | bytes 1048576 | tf_op jit(solution)/shard_map/all_to_all | solution.py:22
  269.2 3.3 %fusion.35 = f32[128,4096]{1,0:T(8,128)} fusion(f32[128,4096]{1,0:T(8,128)S(1)} %fusion.38, f32[128]{0:T(128)S(1)} %maximum_convert_fusion.1, s32[]{:T(128)S(6)} %mul_shard_map.3, s32[128]{0:T(128)S(1)} %iota_shift-right-arithmetic_fusion.1, f32[128]{0:T(128)S(1)} %compare_convert_fusion.4, s32[128]{0:T(128)S(1)} %get-tuple-element.13, ...), kind=kOutput, calls=%fused_computation.50 | convolution fusion | flops 805502976 | bytes 4196484 | tf_op jit(solution)/shard_map/dot_general | solution.py:58
  272.5 4.4 %all-to-all-done.1 = f32[4,1,8,4096]{3,2,1,0:T(8,128)S(1)} async-done(((f32[4,1,8,4096]{3,2,1,0:T(8,128)}), f32[4,1,8,4096]{3,2,1,0:T(8,128)S(1)}, u32[]{:S(2)}, u32[]{:S(2)}) %all-to-all-start.1) | async-done | bytes 524320 | tf_op jit(solution)/shard_map/all_to_all | solution.py:22
  276.9 1.3 fusion.15
  278.1 1.3 fusion.13
  279.4 3.4 %convolution_add_fusion.1 = f32[128,4096]{1,0:T(8,128)S(1)} fusion(f32[128,4096]{1,0:T(8,128)} %fusion.35, f32[1,8,4096]{2,0,1:T(1,128)S(1)} %fusion.15, f32[128]{0:T(128)S(1)} %get-tuple-element.5, s32[128]{0:T(128)S(1)} %get-tuple-element.13), kind=kOutput, calls=%fused_computation.2 | convolution fusion | flops 50857984 | bytes 4326400 | tf_op jit(solution)/shard_map/dot_general | solution.py:58
  282.8 3.2 %fusion = f32[1,128,4096]{2,1,0:T(8,128)} fusion(f32[128,4096]{1,0:T(8,128)S(1)} %convolution_add_fusion.1, f32[1,8,4096]{2,0,1:T(1,128)S(1)} %fusion.13, f32[128]{0:T(128)S(1)} %get-tuple-element.6, s32[128]{0:T(128)S(1)} %get-tuple-element.13), kind=kOutput, calls=%fused_computation.1 | convolution fusion | flops 50857984 | bytes 4326400 | tf_op jit(solution)/shard_map/dot_general | solution.py:58
  (32 shorter events, 3.0 us)
Async XLA Ops:
  18.9 8.4 %copy-start = (s32[1,128]{1,0:T(1,128)S(1)}, s32[1,128]{1,0:T(1,128)}, u32[]{:S(2)}) copy-start(s32[1,128]{1,0:T(1,128)} %param.7) | copy-start | bytes 1540
  21.7 11.8 %all-to-all-start = ((f32[4,1,8,4096]{3,2,1,0:T(8,128)}), f32[4,1,8,4096]{3,2,1,0:T(8,128)S(1)}, u32[]{:S(2)}, u32[]{:S(2)}) async-start(f32[4,1,8,4096]{3,2,1,0:T(8,128)} %broadcast_in_dim.69), calls=%async_computation | async-start | bytes 1048576 | tf_op jit(solution)/shard_map/all_to_all | solution.py:22
  26.6 225.9 %all-reduce.3.cloned.1.call-start = ((), (), s32[]{:S(2)}) async-start(), calls=%async_computation.2 | async-start | bytes 8388608 | tf_op jit(solution)/shard_map/psum | solution.py:105
  265.2 11.6 %all-to-all-start.1 = ((f32[4,1,8,4096]{3,2,1,0:T(8,128)}), f32[4,1,8,4096]{3,2,1,0:T(8,128)S(1)}, u32[]{:S(2)}, u32[]{:S(2)}) async-start(f32[4,1,8,4096]{3,2,1,0:T(8,128)} %broadcast_in_dim.73), calls=%async_computation.1 | async-start | bytes 1048576 | tf_op jit(solution)/shard_map/all_to_all | solution.py:22
Sparse Core Ops, SparseCore 0:
  40.9 211.4 all-reduce.2
where the time goes:
time: 295 us; the launch traced here: 293 us
  waiting for transfers between devices  221 us (75%)
  matrix products  38 us (13%)
  between operations  15 us (5%)
  starting transfers between devices  8.79 us (3%)
  local copies, waits for them, and re-layouts  8.08 us (3%)
    psum x1, waiting for transfers between devices, shards(): total = lax.psum(term, 'grp')  210 us
    dot_general x8, matrix products, exact_dot(): jnp.dot(left, right, precision=lax.Precision.HIGHEST, preferred_element_t...  23.7 us
    all_to_all x2, waiting for transfers between devices, from_everyone(): lax.all_to_all(jnp.broadcast_to(x[None], (length, *x.shape)), axis, 0, 0,...  10.6 us
    all_to_all x2, starting transfers between devices, from_everyone(): lax.all_to_all(jnp.broadcast_to(x[None], (length, *x.shape)), axis, 0, 0,...  8.79 us
    dot_general x2, matrix products, inner_apply(): jnp.einsum('rjk,lk->rjl', shaped, rest_op, precision=lax.Precision.HIGHEST)  6.68 us
  transfers between devices with their start and end apart: 3, of which 3 were waited for; matrix products, arithmetic and copies ran while one was open for 2% of the time, Pallas kernels for 0%

commit v1 on v0

v1 whole, which is shorter than its diff:
```python
import functools

import jax
import jax.numpy as jnp
import numpy as np
from jax import lax
from jax.experimental import pallas as pl
from jax.experimental.pallas import tpu as pltpu
from jax.sharding import PartitionSpec as P

LEVEL_SUM = 9
LOW_LEVEL = 6
NY = 8
NZ = 8
MEMBERS = 8
CROSS = 16
ROWS = 128
PLANE = 8
EXT = 144
BACK = 136
PART = 72
BLOCK = 32
LANES = 128
BLOCKS_OF = {6: (0, 1, 3, 4), 7: (0, 1, 2, 5), 8: (0, 2, 6, 7)}


def place_of(x, y):
    if x % 4 == 0 and y % 4 == 0:
        return (x // 4) * 2 + y // 4
    if x % 4 == 0 and y % 2 == 0:
        return 32 + (x // 4) * 2 + y // 4
    if x % 4 == 2 and y % 4 == 0:
        return 64 + (x // 4) * 2 + y // 4
    if x % 4 == 0:
        return 96 + (x // 4) * 4 + y // 2
    if x % 4 == 2:
        return 160 + (x // 4) * 2 + y // 4
    return 192 + (x // 2) * 2 + y // 4


def hier_line(n):
    h = np.zeros((n, n), np.float32)
    for j in range(n):
        h[j, j] += 1.0
        if j:
            s = j & -j
            h[j, j - s] -= 0.5
            h[j, (j + s) % n] -= 0.5
    return h


def dehier_line(n):
    e = np.zeros((n, n), np.float32)
    e[:, 0] = 1.0
    for k in range(1, n):
        for j in range(n):
            d = min(abs(j - k), n - abs(j - k))
            e[j, k] = max(0.0, 1.0 - d / (k & -k))
    return e


@functools.cache
def row_tables():
    forth = np.zeros((3, EXT, EXT), np.float32)
    back = np.zeros((3, ROWS, EXT), np.float32)
    for level in (6, 7, 8):
        n = 1 << (LEVEL_SUM - level)
        span = ROWS // n
        hy, ey = hier_line(n), dehier_line(n)
        blocks = BLOCKS_OF[level]
        f, g = forth[level - LOW_LEVEL], back[level - LOW_LEVEL]
        for i in range(span):
            for y in range(n):
                t = place_of(i * 64 // span, y * 8 // n)
                m = BLOCK * blocks.index(t // BLOCK) + t % BLOCK
                s = i & -i
                steps = [(i, 1.0)] + ([(i - s, -0.5), (i + s, -0.5)] if i else [])
                for j, w in steps:
                    f[m, j * n : j * n + n] += w * hy[y]
                for j in range(span):
                    w = max(0.0, 1.0 - abs(j - i) / s) if i else 1.0 - j / span
                    g[j * n : j * n + n, m] += w * ey[:, y]
        for y in range(n):
            t = ROWS + y * 8 // n
            f[t, ROWS : ROWS + n] += hy[y]
            for j in range(span):
                g[j * n : j * n + n, t] += j / span * ey[:, y]
    return forth, back


def two_part_dot(table, values):
    high = values.astype(jnp.bfloat16)
    low = (values - high.astype(jnp.float32)).astype(jnp.bfloat16)
    dot = functools.partial(jnp.dot, preferred_element_type=jnp.float32)
    return dot(table, high) + dot(table, low)


def forth_kernel(level_ref, table_ref, rows_ref, next_ref, out_ref):
    width = rows_ref.shape[1]
    values = jnp.concatenate(
        [rows_ref[...], next_ref[...], jnp.zeros((EXT - BACK, width), jnp.float32)], axis=0
    )
    out_ref[0] = two_part_dot(table_ref[...], values)
    level = jnp.broadcast_to(level_ref[0], (EXT - BACK, width))
    out_ref[0, BACK:EXT, :] = level.astype(jnp.float32)


def add_kernel(got_ref, out_ref):
    sums = [None] * 8

    def add(block, value):
        sums[block] = value if sums[block] is None else sums[block] + value

    there = None
    for k in range(MEMBERS):
        level = got_ref[k, BACK : BACK + 1, :]
        six, seven, eight = level == 6.0, level == 7.0, level == 8.0
        first, second, third, fourth = (
            got_ref[k, BLOCK * i : BLOCK * (i + 1), :] for i in range(4)
        )
        add(0, first)
        add(1, jnp.where(eight, 0.0, second))
        add(2, jnp.where(eight, second, jnp.where(seven, third, 0.0)))
        add(3, jnp.where(six, third, 0.0))
        add(4, jnp.where(six, fourth, 0.0))
        add(5, jnp.where(seven, fourth, 0.0))
        add(6, jnp.where(eight, third, 0.0))
        add(7, jnp.where(eight, fourth, 0.0))
        part = got_ref[k, ROWS:BACK, :]
        there = part if there is None else there + part
    pad = jnp.zeros((4 * PART - 8 * BLOCK - PLANE, there.shape[1]), jnp.float32)
    table = jnp.concatenate([*sums, there, pad], axis=0)
    for q in range(4):
        out_ref[q] = table[q * PART : (q + 1) * PART]


def total_kernel(got_ref, out_ref):
    total = got_ref[0]
    for k in range(1, CROSS):
        total = total + got_ref[k]
    for k in range(CROSS):
        out_ref[k] = total


def pick_kernel(table_ref, level_ref, out_ref):
    table = jnp.concatenate([table_ref[q] for q in range(4)], axis=0)
    blocks = [table[BLOCK * i : BLOCK * (i + 1)] for i in range(8)]
    for k in range(MEMBERS):
        level = level_ref[k, 0:1, :]
        six, eight = level == 6.0, level == 8.0
        out_ref[k, 0:32, :] = blocks[0]
        out_ref[k, 32:64, :] = jnp.where(eight, blocks[2], blocks[1])
        out_ref[k, 64:96, :] = jnp.where(six, blocks[3], jnp.where(eight, blocks[6], blocks[2]))
        out_ref[k, 96:128, :] = jnp.where(six, blocks[4], jnp.where(eight, blocks[7], blocks[5]))
        out_ref[k, 128:136, :] = table[256:264]


def back_kernel(table_ref, got_ref, out_ref):
    width = got_ref.shape[2]
    values = jnp.concatenate(
        [got_ref[0], jnp.zeros((EXT - BACK, width), jnp.float32)], axis=0
    )
    out_ref[...] = two_part_dot(table_ref[...], values)


def member(y, z, core):
    return (y * NZ + z) * 2 + core


LINES = [[member(y, z, 0) for y in range(NY)] for z in range(NZ)] + [
    [member(y, z, 1) for z in range(NZ)] for y in range(NY)
]
CROSSES = [
    [member(k, z, 0) for z in range(NZ)] + [member(y, k, 1) for y in range(NY)]
    for k in range(MEMBERS)
]


def exchange(values, groups):
    return lax.all_to_all(values, "grp", 0, 0, axis_index_groups=groups, tiled=True)


def f32(*shape):
    return jax.ShapeDtypeStruct(shape, jnp.float32)


def shards(grids, first_level, coeffs, slot_map):
    rows = grids[0]
    width = rows.shape[1]
    chunk = width // MEMBERS
    lanes = chunk // LANES
    slabs = lax.axis_size("slab")
    following = lax.ppermute(
        rows[:PLANE], "slab", [(i, (i - 1) % slabs) for i in range(slabs)]
    )
    forth, back = row_tables()
    which = first_level[0] - LOW_LEVEL
    pick = lambda tables: lax.dynamic_index_in_dim(
        jnp.asarray(tables, jnp.bfloat16), which, 0, keepdims=False
    )
    forth_table = pick(forth) * coeffs[0].astype(jnp.bfloat16)
    back_table = pick(back)
    whole = lambda shape: pl.BlockSpec(shape, lambda *_: (0,) * len(shape))

    sent = pl.pallas_call(
        forth_kernel,
        grid=(MEMBERS,),
        in_specs=[
            pl.BlockSpec(memory_space=pltpu.SMEM),
            whole((EXT, EXT)),
            pl.BlockSpec((ROWS, chunk), lambda k: (0, k)),
            pl.BlockSpec((PLANE, chunk), lambda k: (0, k)),
        ],
        out_specs=pl.BlockSpec((1, EXT, chunk), lambda k: (k, 0, 0)),
        out_shape=f32(MEMBERS, EXT, chunk),
        name="forth",
    )(first_level, forth_table, rows, following)
    got = exchange(sent, LINES)

    parts = pl.pallas_call(
        add_kernel,
        grid=(lanes,),
        in_specs=[pl.BlockSpec((MEMBERS, EXT, LANES), lambda j: (0, 0, j))],
        out_specs=pl.BlockSpec((4, PART, LANES), lambda j: (j, 0, 0)),
        out_shape=f32(CROSS, PART, LANES),
        name="add",
    )(got)
    parts = exchange(parts, CROSSES)

    total = pl.pallas_call(
        total_kernel,
        out_shape=f32(CROSS, PART, LANES),
        name="total",
    )(parts)
    table = exchange(total, CROSSES)

    picked = pl.pallas_call(
        pick_kernel,
        grid=(lanes,),
        in_specs=[
            pl.BlockSpec((4, PART, LANES), lambda j: (j, 0, 0)),
            pl.BlockSpec((MEMBERS, PLANE, LANES), lambda j: (0, BACK // PLANE, 0)),
        ],
        out_specs=pl.BlockSpec((MEMBERS, BACK, LANES), lambda j: (0, 0, j)),
        out_shape=f32(MEMBERS, BACK, chunk),
        name="pick",
    )(table, got)
    final = exchange(picked, LINES)

    out = pl.pallas_call(
        back_kernel,
        grid=(MEMBERS,),
        in_specs=[
            whole((ROWS, EXT)),
            pl.BlockSpec((1, BACK, chunk), lambda k: (k, 0, 0)),
        ],
        out_specs=pl.BlockSpec((ROWS, chunk), lambda k: (0, k)),
        out_shape=f32(ROWS, width),
        name="back",
    )(back_table, final)
    return out[None]


def solution(mesh):
    in_specs = (P("grp", "slab", None), P("grp"), P("grp"), P("grp", "slab"))
    out_specs = P("grp", "slab", None)
    return jax.shard_map(shards, mesh=mesh, in_specs=in_specs, out_specs=out_specs, check_vma=False)
```

time: 295 us -> 176 us (0.60)
  the two profiles are of different devices: /device:TPU:1 before, /device:TPU:6 now
where the time goes in v1:
time: 176 us; the launch traced here: 175 us
  blocking collectives  97.4 us (55%)
  waiting for transfers between devices  35.3 us (20%)
  Pallas kernels  22.2 us (13%)
  starting transfers between devices  13.2 us (8%)
  local copies, waits for them, and re-layouts  4.4 us (3%)
    all_to_all x3, blocking collectives, exchange(): lax.all_to_all(values, 'grp', 0, 0, axis_index_groups=groups, tiled=True)  97.4 us
    all_to_all x1, waiting for transfers between devices, exchange(): lax.all_to_all(values, 'grp', 0, 0, axis_index_groups=groups, tiled=True)  30.2 us
    all_to_all x1, starting transfers between devices, exchange(): lax.all_to_all(values, 'grp', 0, 0, axis_index_groups=groups, tiled=True)  10.5 us
    pallas_call x1, Pallas kernels, shards(): pl.pallas_call(forth_kernel, grid=(MEMBERS,), in_specs=[pl.BlockSpec(memo...  6.55 us
    pallas_call x1, Pallas kernels, shards(): pl.pallas_call(back_kernel, grid=(MEMBERS,), in_specs=[whole((ROWS, EXT))...  6.43 us
    ppermute x1, waiting for transfers between devices, shards(): lax.ppermute(rows[:PLANE], 'slab', [(i, (i - 1) % slabs) for i in range(s...  5.1 us
    pallas_call x1, Pallas kernels, shards(): pl.pallas_call(add_kernel, grid=(lanes,), in_specs=[pl.BlockSpec((MEMBERS...  3.67 us
    pallas_call x1, Pallas kernels, shards(): pl.pallas_call(pick_kernel, grid=(lanes,), in_specs=[pl.BlockSpec((4, PAR...  3.58 us
  transfers between devices with their start and end apart: 2, of which 2 were waited for; matrix products, arithmetic and copies ran while one was open for 2% of the time, Pallas kernels for 0%

profile of v1, /device:TPU:6, one launch (start us, length us, event | category | flops | bytes accessed | tf_op | source)
XLA Modules:
  0.0 175.3 jit_solution(3049292694434837809)
XLA Ops:
  0.0 0.9 slice_bitcast_fusion
  0.9 2.7 %collective-permute-start = (f32[8,4096]{1,0:T(8,128)S(1)}, f32[8,4096]{1,0:T(8,128)S(1)}, u32[]{:S(2)}, u32[]{:S(2)}) collective-permute-start(f32[8,4096]{1,0:T(8,128)S(1)} %slice_bitcast_fusion), channel_id=1, source_target_pairs={{0,3},{1,0},{2,1},{3,2},{4,7},{5,4},{6,5},{7,6},{8,11},{9,8},{10,9... | collective-permute-start | bytes 393224 | tf_op jit(solution)/shard_map/ppermute | solution.py:193
  5.0 1.5 multiply_bitcast_fusion.table_ref
  6.5 5.1 %collective-permute-done.next_ref = f32[8,4096]{1,0:T(8,128)S(1)} collective-permute-done((f32[8,4096]{1,0:T(8,128)S(1)}, f32[8,4096]{1,0:T(8,128)S(1)}, u32[]{:S(2)}, u32[]{:S(2)}) %collective-permute-start) | collective-permute-done | bytes 131104 | tf_op jit(solution)/shard_map/ppermute | solution.py:193
  11.6 0.0 copy-start.1
  11.6 0.7 copy-done.1
  12.2 6.5 %forth.1 = f32[8,144,512]{2,1,0:T(8,128)} custom-call(s32[1]{0:T(128)S(6)} %copy.6.level_ref, bf16[144,144]{1,0:T(8,128)(2,1)} %multiply_bitcast_fusion.table_ref, f32[128,4096]{1,0:T(8,128)} %bitcast.11, f32[8,4096]{1,0:T(8,128)} %copy-done.1), custom_call_target="tpu_custom_call" | custom-call | tf_op jit(solution)/shard_map/forth/pallas_call | solution.py:205
  18.8 37.8 %all_to_all.20.got_ref.level_ref = f32[8,144,512]{2,1,0:T(8,128)} all-to-all(f32[8,144,512]{2,1,0:T(8,128)} %forth.1), channel_id=1, replica_groups={{0,64,128,192,256,320,384,448},{8,72,136,200,264,328,392,456},{16,80,14..., dimensions={0} | all-to-all | bytes 4718592 | tf_op jit(solution)/shard_map/all_to_all | solution.py:180
  56.6 3.7 %add.16 = f32[16,72,128]{2,1,0:T(8,128)} custom-call(f32[8,144,512]{2,1,0:T(8,128)} %all_to_all.20.got_ref.level_ref), custom_call_target="tpu_custom_call" | custom-call | tf_op jit(solution)/shard_map/add/pallas_call | solution.py:220
  60.3 30.5 %all_to_all.21.got_ref = f32[16,72,128]{2,1,0:T(8,128)} all-to-all(f32[16,72,128]{2,1,0:T(8,128)} %add.16), channel_id=1, replica_groups={{0,8,16,24,32,40,48,56,4,68,132,196,260,324,388,452},{64,72,80,88,96,10..., dimensions={0} | all-to-all | bytes 1179648 | tf_op jit(solution)/shard_map/all_to_all | solution.py:180
  90.8 1.9 %total.1 = f32[16,72,128]{2,1,0:T(8,128)} custom-call(f32[16,72,128]{2,1,0:T(8,128)} %all_to_all.21.got_ref), custom_call_target="tpu_custom_call" | custom-call | tf_op jit(solution)/shard_map/total/pallas_call | solution.py:230
  92.8 29.0 %all_to_all.22.table_ref = f32[16,72,128]{2,1,0:T(8,128)} all-to-all(f32[16,72,128]{2,1,0:T(8,128)} %total.1), channel_id=1, replica_groups={{0,8,16,24,32,40,48,56,4,68,132,196,260,324,388,452},{64,72,80,88,96,10..., dimensions={0} | all-to-all | bytes 1179648 | tf_op jit(solution)/shard_map/all_to_all | solution.py:180
  121.8 3.6 %pick.1 = f32[8,136,512]{2,1,0:T(8,128)} custom-call(f32[16,72,128]{2,1,0:T(8,128)} %all_to_all.22.table_ref, f32[8,144,512]{2,1,0:T(8,128)} %all_to_all.20.got_ref.level_ref), custom_call_target="tpu_custom_call" | custom-call | tf_op jit(solution)/shard_map/pick/pallas_call | solution.py:237
  125.3 10.5 %all-to-all-start.3 = ((f32[8,136,512]{2,1,0:T(8,128)}), f32[8,136,512]{2,1,0:T(8,128)S(1)}, u32[]{:S(2)}, u32[]{:S(2)}) async-start(f32[8,136,512]{2,1,0:T(8,128)} %pick.1), calls=%async_computation.3 | async-start | bytes 4456448 | tf_op jit(solution)/shard_map/all_to_all | solution.py:180
  135.8 1.5 dynamic-slice_bitcast_fusion.table_ref
  137.3 30.2 %all-to-all-done.3.got_ref = f32[8,136,512]{2,1,0:T(8,128)S(1)} async-done(((f32[8,136,512]{2,1,0:T(8,128)}), f32[8,136,512]{2,1,0:T(8,128)S(1)}, u32[]{:S(2)}, u32[]{:S(2)}) %all-to-all-start.3) | async-done | bytes 2228256 | tf_op jit(solution)/shard_map/all_to_all | solution.py:180
  167.5 0.0 copy-start
  167.5 1.4 copy-done
  168.9 6.4 %back.1 = f32[128,4096]{1,0:T(8,128)} custom-call(bf16[128,144]{1,0:T(8,128)(2,1)} %dynamic-slice_bitcast_fusion.table_ref, f32[8,136,512]{2,1,0:T(8,128)} %copy-done), custom_call_target="tpu_custom_call" | custom-call | tf_op jit(solution)/shard_map/back/pallas_call | solution.py:250
Async XLA Ops:
  0.9 10.7 %collective-permute-start = (f32[8,4096]{1,0:T(8,128)S(1)}, f32[8,4096]{1,0:T(8,128)S(1)}, u32[]{:S(2)}, u32[]{:S(2)}) collective-permute-start(f32[8,4096]{1,0:T(8,128)S(1)} %slice_bitcast_fusion), channel_id=1, source_target_pairs={{0,3},{1,0},{2,1},{3,2},{4,7},{5,4},{6,5},{7,6},{8,11},{9,8},{10,9... | collective-permute-start | bytes 393224 | tf_op jit(solution)/shard_map/ppermute | solution.py:193
  11.6 0.7 copy-start.1
  125.3 42.2 %all-to-all-start.3 = ((f32[8,136,512]{2,1,0:T(8,128)}), f32[8,136,512]{2,1,0:T(8,128)S(1)}, u32[]{:S(2)}, u32[]{:S(2)}) async-start(f32[8,136,512]{2,1,0:T(8,128)} %pick.1), calls=%async_computation.3 | async-start | bytes 4456448 | tf_op jit(solution)/shard_map/all_to_all | solution.py:180
  167.5 1.4 copy-start

commit v2 on v1

v2 whole, which is shorter than its diff:
```python
import functools

import jax
import jax.numpy as jnp
import numpy as np
from jax import lax
from jax.experimental import pallas as pl
from jax.experimental.pallas import tpu as pltpu
from jax.sharding import PartitionSpec as P

LEVEL_SUM = 9
LOW_LEVEL = 6
NY = 8
NZ = 8
MEMBERS = 8
ROWS = 128
PLANE = 8
BLOCK = 32
SLOTS = 7
THERE = SLOTS * BLOCK
FLAGS = THERE + PLANE
SENT = FLAGS + 8
ENTRY = 2 * (ROWS + PLANE)
PART = 72
LANES = 128
BLOCKS_OF = {6: (0, 1, 3, 4), 7: (0, 1, 2, 5), 8: (0, 2, 6, 7)}


def slots_of(levels):
    six, seven, eight = (level in levels for level in (6, 7, 8))
    third = 3 if six else (5 if seven else None)
    fifth = 6 if eight else (5 if six and seven else None)
    return (0, 1, 2, third, 4, fifth, 7)


def place_of(x, y):
    if x % 4 == 0 and y % 4 == 0:
        return (x // 4) * 2 + y // 4
    if x % 4 == 0 and y % 2 == 0:
        return 32 + (x // 4) * 2 + y // 4
    if x % 4 == 2 and y % 4 == 0:
        return 64 + (x // 4) * 2 + y // 4
    if x % 4 == 0:
        return 96 + (x // 4) * 4 + y // 2
    if x % 4 == 2:
        return 160 + (x // 4) * 2 + y // 4
    return 192 + (x // 2) * 2 + y // 4


def hier_line(n):
    h = np.zeros((n, n), np.float32)
    for j in range(n):
        h[j, j] += 1.0
        if j:
            s = j & -j
            h[j, j - s] -= 0.5
            h[j, (j + s) % n] -= 0.5
    return h


def dehier_line(n):
    e = np.zeros((n, n), np.float32)
    e[:, 0] = 1.0
    for k in range(1, n):
        for j in range(n):
            d = min(abs(j - k), n - abs(j - k))
            e[j, k] = max(0.0, 1.0 - d / (k & -k))
    return e


def one_grid(level, slots):
    n = 1 << (LEVEL_SUM - level)
    span = ROWS // n
    hy, ey = hier_line(n), dehier_line(n)
    forth = np.zeros((SENT, ROWS + PLANE), np.float32)
    back = np.zeros((ROWS, SENT), np.float32)
    for i in range(span):
        for y in range(n):
            t = place_of(i * 64 // span, y * 8 // n)
            m = BLOCK * slots.index(t // BLOCK) + t % BLOCK
            s = i & -i
            steps = [(i, 1.0)] + ([(i - s, -0.5), (i + s, -0.5)] if i else [])
            for j, w in steps:
                forth[m, j * n : j * n + n] += w * hy[y]
            for j in range(span):
                w = max(0.0, 1.0 - abs(j - i) / s) if i else 1.0 - j / span
                back[j * n : j * n + n, m] += w * ey[:, y]
    for y in range(n):
        t = THERE + y * 8 // n
        forth[t, ROWS : ROWS + n] += hy[y]
        for j in range(span):
            back[j * n : j * n + n, t] += j / span * ey[:, y]
    return forth, back


@functools.cache
def row_tables():
    forth, back = [], []
    for own in (6, 7, 8):
        for other in (6, 7, 8):
            slots = slots_of((own, other))
            mine, theirs = one_grid(own, slots), one_grid(other, slots)
            forth.append(np.concatenate([mine[0], theirs[0]], axis=1))
            back.append(mine[1])
    return np.stack(forth), np.stack(back)


def two_part_dot(table, values):
    high = values.astype(jnp.bfloat16)
    low = (values - high.astype(jnp.float32)).astype(jnp.bfloat16)
    dot = functools.partial(jnp.dot, preferred_element_type=jnp.float32)
    return dot(table, high) + dot(table, low)


def number_in(ref, row):
    return jnp.max(ref[row : row + 1, :LANES])


def forth_kernel(core_ref, level_ref, coeff_ref, table_ref, own_ref, own_next_ref, other_ref, other_next_ref, out_ref):
    own_level = level_ref[0]
    other_level = number_in(other_next_ref, PLANE).astype(jnp.int32)
    own_coeff = coeff_ref[0].astype(jnp.float32)
    other_coeff = other_next_ref[PLANE + 1 : PLANE + 2, :]
    which = (own_level - LOW_LEVEL) * 3 + other_level - LOW_LEVEL
    values = jnp.concatenate(
        [
            own_ref[...] * own_coeff,
            own_next_ref[...] * own_coeff,
            other_ref[...] * other_coeff,
            other_next_ref[:PLANE] * other_coeff,
        ],
        axis=0,
    )
    out_ref[0] = two_part_dot(table_ref[which], values)
    six = jnp.logical_or(own_level == 6, other_level == 6).astype(jnp.float32)
    eight = jnp.logical_or(own_level == 8, other_level == 8).astype(jnp.float32)
    line = lax.broadcasted_iota(jnp.int32, (SENT - FLAGS, values.shape[1]), 0)
    out_ref[0, FLAGS:SENT, :] = jnp.where(line == 0, six, eight)


def add_kernel(got_ref, out_ref):
    sums = [None] * 9

    def add(block, value):
        sums[block] = value if sums[block] is None else sums[block] + value

    for k in range(MEMBERS):
        six = got_ref[k, FLAGS : FLAGS + 1, :] == 1.0
        eight = got_ref[k, FLAGS + 1 : FLAGS + 2, :] == 1.0
        slot = [got_ref[k, BLOCK * i : BLOCK * (i + 1), :] for i in range(SLOTS)]
        add(0, slot[0])
        add(1, slot[1])
        add(2, slot[2])
        add(3, jnp.where(six, slot[3], 0.0))
        add(4, slot[4])
        add(5, jnp.where(six, jnp.where(eight, 0.0, slot[5]), slot[3]))
        add(6, jnp.where(eight, slot[5], 0.0))
        add(7, slot[6])
        add(8, got_ref[k, THERE:FLAGS, :])
    pad = jnp.zeros((4 * PART - 8 * BLOCK - PLANE, sums[0].shape[1]), jnp.float32)
    table = jnp.concatenate([*sums, pad], axis=0)
    for q in range(4):
        out_ref[q] = table[q * PART : (q + 1) * PART]


def total_kernel(got_ref, out_ref):
    total = got_ref[0]
    for k in range(1, MEMBERS):
        total = total + got_ref[k]
    for k in range(MEMBERS):
        out_ref[k] = total


def pick_kernel(table_ref, flags_ref, out_ref):
    table = jnp.concatenate([table_ref[q] for q in range(4)], axis=0)
    blocks = [table[BLOCK * i : BLOCK * (i + 1)] for i in range(8)]
    for k in range(MEMBERS):
        six = flags_ref[k, 0:1, :] == 1.0
        eight = flags_ref[k, 1:2, :] == 1.0
        slots = (
            blocks[0],
            blocks[1],
            blocks[2],
            jnp.where(six, blocks[3], blocks[5]),
            blocks[4],
            jnp.where(eight, blocks[6], blocks[5]),
            blocks[7],
        )
        for i, slot in enumerate(slots):
            out_ref[k, BLOCK * i : BLOCK * (i + 1), :] = slot
        out_ref[k, THERE:FLAGS, :] = table[8 * BLOCK : 8 * BLOCK + PLANE]


def back_kernel(core_ref, level_ref, meta_ref, table_ref, got_ref, *rest):
    out_ref = rest[-1]
    other_level = number_in(meta_ref, 0).astype(jnp.int32)
    which = (level_ref[0] - LOW_LEVEL) * 3 + other_level - LOW_LEVEL
    values = jnp.concatenate(
        [got_ref[0], jnp.zeros((SENT - FLAGS, got_ref.shape[2]), jnp.float32)], axis=0
    )
    out_ref[...] = two_part_dot(table_ref[which], values)


def member(y, z, core):
    return (y * NZ + z) * 2 + core


ALONG_Y = [[[member(y, z, core) for y in range(NY)] for z in range(NZ)] for core in (0, 1)]
ALONG_Z = [[[member(y, z, core) for z in range(NZ)] for y in range(NY)] for core in (0, 1)]
FIRST = ALONG_Y[0] + ALONG_Z[1]
SECOND = ALONG_Z[0] + ALONG_Y[1]


def exchange(values, groups):
    return lax.all_to_all(values, "grp", 0, 0, axis_index_groups=groups, tiled=True)


def f32(*shape):
    return jax.ShapeDtypeStruct(shape, jnp.float32)


def shards(grids, first_level, coeffs, slot_map):
    rows = grids[0]
    width = rows.shape[1]
    half = width // 2
    chunk = half // MEMBERS
    lanes = chunk // LANES
    slabs = lax.axis_size("slab")
    members = lax.axis_size("grp")
    core = lax.axis_index("grp") % 2
    swap = [(i, i ^ 1) for i in range(members)]
    mine, theirs = core * half, (1 - core) * half

    def to_previous(values, turn):
        pairs = [
            (g * slabs + s, (g ^ turn) * slabs + (s - 1) % slabs)
            for g in range(members)
            for s in range(slabs)
        ]
        return lax.ppermute(values, ("grp", "slab"), pairs)

    numbers = jnp.concatenate(
        [
            jnp.broadcast_to(first_level.astype(jnp.float32)[:, None], (1, half)),
            jnp.broadcast_to(coeffs.astype(jnp.float32)[:, None], (PLANE - 1, half)),
        ],
        axis=0,
    )
    plane = rows[:PLANE]
    other_next = to_previous(
        jnp.concatenate([lax.dynamic_slice_in_dim(plane, theirs, half, 1), numbers], axis=0), 1
    )
    own_next = to_previous(lax.dynamic_slice_in_dim(plane, mine, half, 1), 0)
    other = lax.ppermute(lax.dynamic_slice_in_dim(rows, theirs, half, 1), "grp", swap)

    forth, back = row_tables()
    forth = jnp.asarray(forth, jnp.bfloat16)
    back = jnp.asarray(back, jnp.bfloat16)
    cores = core.astype(jnp.int32)[None]
    whole = lambda shape: pl.BlockSpec(shape, lambda *_: (0,) * len(shape))
    smem = pl.BlockSpec(memory_space=pltpu.SMEM)

    sent = pl.pallas_call(
        forth_kernel,
        grid_spec=pltpu.PrefetchScalarGridSpec(
            num_scalar_prefetch=1,
            grid=(MEMBERS,),
            in_specs=[
                smem,
                smem,
                whole((9, SENT, ENTRY)),
                pl.BlockSpec((ROWS, chunk), lambda k, c: (0, c[0] * MEMBERS + k)),
                pl.BlockSpec((PLANE, chunk), lambda k, c: (0, k)),
                pl.BlockSpec((ROWS, chunk), lambda k, c: (0, k)),
                pl.BlockSpec((2 * PLANE, chunk), lambda k, c: (0, k)),
            ],
            out_specs=pl.BlockSpec((1, SENT, chunk), lambda k, c: (k, 0, 0)),
        ),
        out_shape=f32(MEMBERS, SENT, chunk),
        name="forth",
    )(cores, first_level, coeffs, forth, rows, own_next, other, other_next)
    got = exchange(sent, FIRST)

    parts = pl.pallas_call(
        add_kernel,
        grid=(lanes,),
        in_specs=[pl.BlockSpec((MEMBERS, SENT, LANES), lambda j: (0, 0, j))],
        out_specs=pl.BlockSpec((4, PART, LANES), lambda j: (j, 0, 0)),
        out_shape=f32(4 * lanes, PART, LANES),
        name="add",
    )(got)
    parts = exchange(parts, SECOND)

    total = pl.pallas_call(
        total_kernel,
        out_shape=f32(MEMBERS, PART, LANES),
        name="total",
    )(parts)
    table = exchange(total, SECOND)

    picked = pl.pallas_call(
        pick_kernel,
        grid=(lanes,),
        in_specs=[
            pl.BlockSpec((4, PART, LANES), lambda j: (j, 0, 0)),
            pl.BlockSpec((MEMBERS, SENT - FLAGS, LANES), lambda j: (0, FLAGS // 8, 0)),
        ],
        out_specs=pl.BlockSpec((MEMBERS, FLAGS, LANES), lambda j: (0, 0, j)),
        out_shape=f32(MEMBERS, FLAGS, chunk),
        name="pick",
    )(table, got)
    final = exchange(picked, FIRST)
    final_other = lax.ppermute(final, "grp", swap)

    def rebuild(values, turn, *filled):
        return pl.pallas_call(
            back_kernel,
            grid_spec=pltpu.PrefetchScalarGridSpec(
                num_scalar_prefetch=1,
                grid=(MEMBERS,),
                in_specs=[
                    smem,
                    pl.BlockSpec((PLANE, LANES), lambda k, c: (1, 0)),
                    whole((9, ROWS, SENT)),
                    pl.BlockSpec((1, FLAGS, chunk), lambda k, c: (k, 0, 0)),
                    *[pl.BlockSpec(memory_space=pl.ANY) for _ in filled],
                ],
                out_specs=pl.BlockSpec(
                    (ROWS, chunk), lambda k, c: (0, (c[0] ^ turn) * MEMBERS + k)
                ),
            ),
            out_shape=f32(ROWS, width),
            input_output_aliases={5: 0} if filled else {},
            cost_estimate=pl.CostEstimate(
                flops=2 * ROWS * SENT * half * 2, bytes_accessed=4 * half * (FLAGS + ROWS), transcendentals=0
            ),
            name="back",
        )(cores, first_level, other_next, back, values, *filled)

    out = rebuild(final_other, 1, rebuild(final, 0))
    return out[None]


def solution(mesh):
    in_specs = (P("grp", "slab", None), P("grp"), P("grp"), P("grp", "slab"))
    out_specs = P("grp", "slab", None)
    return jax.shard_map(shards, mesh=mesh, in_specs=in_specs, out_specs=out_specs, check_vma=False)
```

time: 176 us -> 152 us (0.86)
  the two profiles are of different devices: /device:TPU:6 before, /device:TPU:1 now
where the time goes in v2:
time: 152 us; the launch traced here: 151 us
  blocking collectives  94.4 us (62%)
  Pallas kernels  27.4 us (18%)
  starting transfers between devices  21.3 us (14%)
  waiting for transfers between devices  4.18 us (3%)
  local copies, waits for them, and re-layouts  2.57 us (2%)
    all_to_all x4, blocking collectives, exchange(): lax.all_to_all(values, 'grp', 0, 0, axis_index_groups=groups, tiled=True)  94.4 us
    pallas_call x2, Pallas kernels, rebuild(): pl.pallas_call(back_kernel, grid_spec=pltpu.PrefetchScalarGridSpec(num_sc...  13.4 us
    ppermute x1, starting transfers between devices, shards(): lax.ppermute(lax.dynamic_slice_in_dim(rows, theirs, half, 1), 'grp', swap)  8.75 us
    ppermute x1, starting transfers between devices, shards(): final_other = lax.ppermute(final, 'grp', swap)  8.7 us
    pallas_call x1, Pallas kernels, shards(): pl.pallas_call(forth_kernel, grid_spec=pltpu.PrefetchScalarGridSpec(num_s...  7.85 us
    ppermute x2, waiting for transfers between devices, to_previous(): return lax.ppermute(values, ('grp', 'slab'), pairs)  4.18 us
    ppermute x2, starting transfers between devices, to_previous(): return lax.ppermute(values, ('grp', 'slab'), pairs)  3.84 us
  transfers between devices with their start and end apart: 4, of which 1 were waited for; matrix products, arithmetic and copies ran while one was open for 0% of the time, Pallas kernels for 4%

profile of v2, /device:TPU:1, one launch (start us, length us, event | category | flops | bytes accessed | tf_op | source)
XLA Modules:
  0.0 151.2 jit_solution(18202746131645831296)
XLA Ops:
  0.0 1.4 dynamic-slice_bitcast_fusion
  1.4 8.7 %collective-permute-start.2 = (f32[128,2048]{1,0:T(8,128)S(1)}, f32[128,2048]{1,0:T(8,128)S(1)}, u32[]{:S(2)}, u32[]{:S(2)}) collective-permute-start(f32[128,2048]{1,0:T(8,128)S(1)} %dynamic-slice_bitcast_fusion), channel_id=1, source_target_pairs={{0,4},{4,0},{8,12},{12,8},{16,20},{20,16},{24,28},{28,24},{32,36},... | collective-permute-start | bytes 3145736 | tf_op jit(solution)/shard_map/ppermute | solution.py:254
  11.4 0.1 pad.1.clone
  11.5 0.1 pad.2.clone
  11.6 0.1 maximum_maximum_fusion
  11.7 1.9 %collective-permute-start = (f32[16,2048]{1,0:T(8,128)S(1)}, f32[16,2048]{1,0:T(8,128)S(1)}, u32[]{:S(2)}, u32[]{:S(2)}) collective-permute-start(f32[16,2048]{1,0:T(8,128)S(1)} %maximum_maximum_fusion), channel_id=1, source_target_pairs={{0,7},{1,4},{2,5},{3,6},{4,3},{5,0},{6,1},{7,2},{8,15},{9,12},{10,... | collective-permute-start | bytes 393224 | tf_op jit(solution)/shard_map/ppermute | solution.py:240
  13.6 1.9 %collective-permute-start.1 = (f32[8,2048]{1,0:T(8,128)S(1)}, f32[8,2048]{1,0:T(8,128)S(1)}, u32[]{:S(2)}, u32[]{:S(2)}) collective-permute-start(f32[8,2048]{1,0:T(8,128)S(1)} %get-tuple-element.5), channel_id=1, source_target_pairs={{0,3},{1,0},{2,1},{3,2},{4,7},{5,4},{6,5},{7,6},{8,11},{9,8},{10,9... | collective-permute-start | bytes 196616 | tf_op jit(solution)/shard_map/ppermute | solution.py:240
  15.5 4.2 %collective-permute-done.1.own_next_ref = f32[8,2048]{1,0:T(8,128)S(1)} collective-permute-done((f32[8,2048]{1,0:T(8,128)S(1)}, f32[8,2048]{1,0:T(8,128)S(1)}, u32[]{:S(2)}, u32[]{:S(2)}) %collective-permute-start.1) | collective-permute-done | bytes 65568 | tf_op jit(solution)/shard_map/ppermute | solution.py:240
  19.7 0.0 collective-permute-done.other_next_ref.meta_ref
  19.7 0.0 collective-permute-done.2.other_ref
  19.7 0.6 copy-done.3
  20.4 0.1 copy-done.1
  20.4 0.3 copy-done.2
  20.8 7.9 %forth.1 = f32[8,240,256]{2,1,0:T(8,128)} custom-call(s32[1]{0:T(128)} %bitcast.core_ref, s32[1]{0:T(128)S(6)} %copy.8.level_ref, s32[1]{0:T(128)S(6)} %copy.9.coeff_ref, bf16[9,240,272]{2,1,0:T(8,128)(2,1)} %constant.32.clone.table_ref, f32[128,4096]{1,0:T(8,128)} %bitcast.11, f32[8,2048]{1,0:T(8,128)} %copy-done.3, f32[128,2048]{1,0:T(8,128)} %copy-done.2, ...), custom_call_target="tpu_custom_call" | custom-call | tf_op jit(solution)/shard_map/forth/pallas_call | solution.py:263
  28.6 33.7 %all_to_all.20.got_ref.flags_ref = f32[8,240,256]{2,1,0:T(8,128)} all-to-all(f32[8,240,256]{2,1,0:T(8,128)} %forth.1), channel_id=1, replica_groups={{0,64,128,192,256,320,384,448},{8,72,136,200,264,328,392,456},{16,80,14..., dimensions={0} | all-to-all | bytes 3932160 | tf_op jit(solution)/shard_map/all_to_all | solution.py:215
  62.4 2.2 %add.15 = f32[8,72,128]{2,1,0:T(8,128)} custom-call(f32[8,240,256]{2,1,0:T(8,128)} %all_to_all.20.got_ref.flags_ref), custom_call_target="tpu_custom_call" | custom-call | tf_op jit(solution)/shard_map/add/pallas_call | solution.py:284
  64.6 16.5 %all_to_all.21.got_ref = f32[8,72,128]{2,1,0:T(8,128)} all-to-all(f32[8,72,128]{2,1,0:T(8,128)} %add.15), channel_id=1, replica_groups={{0,8,16,24,32,40,48,56},{64,72,80,88,96,104,112,120},{128,136,144,152,1..., dimensions={0} | all-to-all | bytes 589824 | tf_op jit(solution)/shard_map/all_to_all | solution.py:215
  81.1 1.7 %total.1 = f32[8,72,128]{2,1,0:T(8,128)} custom-call(f32[8,72,128]{2,1,0:T(8,128)} %all_to_all.21.got_ref), custom_call_target="tpu_custom_call" | custom-call | tf_op jit(solution)/shard_map/total/pallas_call | solution.py:294
  82.8 13.7 %all_to_all.22.table_ref = f32[8,72,128]{2,1,0:T(8,128)} all-to-all(f32[8,72,128]{2,1,0:T(8,128)} %total.1), channel_id=1, replica_groups={{0,8,16,24,32,40,48,56},{64,72,80,88,96,104,112,120},{128,136,144,152,1..., dimensions={0} | all-to-all | bytes 589824 | tf_op jit(solution)/shard_map/all_to_all | solution.py:215
  96.5 2.2 %pick.1 = f32[8,232,256]{2,1,0:T(8,128)} custom-call(f32[8,72,128]{2,1,0:T(8,128)} %all_to_all.22.table_ref, f32[8,240,256]{2,1,0:T(8,128)} %all_to_all.20.got_ref.flags_ref), custom_call_target="tpu_custom_call" | custom-call | tf_op jit(solution)/shard_map/pick/pallas_call | solution.py:301
  98.8 30.4 %all_to_all.23.got_ref = f32[8,232,256]{2,1,0:T(8,128)S(1)} all-to-all(f32[8,232,256]{2,1,0:T(8,128)} %pick.1), channel_id=1, replica_groups={{0,64,128,192,256,320,384,448},{8,72,136,200,264,328,392,456},{16,80,14..., dimensions={0} | all-to-all | bytes 3801088 | tf_op jit(solution)/shard_map/all_to_all | solution.py:215
  129.2 8.7 %collective-permute-start.3 = (f32[8,232,256]{2,1,0:T(8,128)S(1)}, f32[8,232,256]{2,1,0:T(8,128)}, u32[]{:S(2)}, u32[]{:S(2)}) collective-permute-start(f32[8,232,256]{2,1,0:T(8,128)S(1)} %all_to_all.23.got_ref), channel_id=1, source_target_pairs={{0,4},{4,0},{8,12},{12,8},{16,20},{20,16},{24,28},{28,24},{32,36},... | collective-permute-start | bytes 5701640 | tf_op jit(solution)/shard_map/ppermute | solution.py:313
  137.9 6.7 %back.2.rest_0_ = f32[128,4096]{1,0:T(8,128)} custom-call(s32[1]{0:T(128)} %bitcast.core_ref, s32[1]{0:T(128)S(6)} %copy.8.level_ref, f32[16,2048]{1,0:T(8,128)} %copy-done.1, bf16[9,128,240]{2,1,0:T(8,128)(2,1)} %constant.33.clone.table_ref, f32[8,232,256]{2,1,0:T(8,128)} %copy-done), custom_call_target="tpu_custom_call" | custom-call | flops 251658240 | bytes 2949120 | tf_op jit(solution)/shard_map/back/pallas_call | solution.py:316
  144.6 6.7 %back.3 = f32[128,4096]{1,0:T(8,128)} custom-call(s32[1]{0:T(128)} %bitcast.core_ref, s32[1]{0:T(128)S(6)} %copy.8.level_ref, f32[16,2048]{1,0:T(8,128)} %copy-done.1, bf16[9,128,240]{2,1,0:T(8,128)(2,1)} %constant.33.clone.table_ref, f32[8,232,256]{2,1,0:T(8,128)} %collective-permute-done.3.got_ref, ...), custom_call_target="tpu_custom_call", output_to_operand_aliasing={{}: (5, {})} | custom-call | flops 251658240 | bytes 2949120 | tf_op jit(solution)/shard_map/back/pallas_call | solution.py:316
  (10 shorter events, 0.0 us)
Async XLA Ops:
  0.0 11.6 %slice-start = ((f32[1,128,4096]{2,1,0:T(8,128)}), f32[1,8,4096]{2,1,0:T(8,128)S(1)}, s32[]{:S(2)}) async-start(f32[1,128,4096]{2,1,0:T(8,128)} %param.6), calls=%async_computation.4 | async-start | bytes 262144 | tf_op jit(solution)/shard_map/slice | solution.py:249
  1.4 18.4 %collective-permute-start.2 = (f32[128,2048]{1,0:T(8,128)S(1)}, f32[128,2048]{1,0:T(8,128)S(1)}, u32[]{:S(2)}, u32[]{:S(2)}) collective-permute-start(f32[128,2048]{1,0:T(8,128)S(1)} %dynamic-slice_bitcast_fusion), channel_id=1, source_target_pairs={{0,4},{4,0},{8,12},{12,8},{16,20},{20,16},{24,28},{28,24},{32,36},... | collective-permute-start | bytes 3145736 | tf_op jit(solution)/shard_map/ppermute | solution.py:254
  11.7 8.0 %collective-permute-start = (f32[16,2048]{1,0:T(8,128)S(1)}, f32[16,2048]{1,0:T(8,128)S(1)}, u32[]{:S(2)}, u32[]{:S(2)}) collective-permute-start(f32[16,2048]{1,0:T(8,128)S(1)} %maximum_maximum_fusion), channel_id=1, source_target_pairs={{0,7},{1,4},{2,5},{3,6},{4,3},{5,0},{6,1},{7,2},{8,15},{9,12},{10,... | collective-permute-start | bytes 393224 | tf_op jit(solution)/shard_map/ppermute | solution.py:240
  13.6 6.1 %collective-permute-start.1 = (f32[8,2048]{1,0:T(8,128)S(1)}, f32[8,2048]{1,0:T(8,128)S(1)}, u32[]{:S(2)}, u32[]{:S(2)}) collective-permute-start(f32[8,2048]{1,0:T(8,128)S(1)} %get-tuple-element.5), channel_id=1, source_target_pairs={{0,3},{1,0},{2,1},{3,2},{4,7},{5,4},{6,5},{7,6},{8,11},{9,8},{10,9... | collective-permute-start | bytes 196616 | tf_op jit(solution)/shard_map/ppermute | solution.py:240
  19.7 0.6 copy-start.3
  19.7 0.7 copy-start.1
  19.7 1.0 copy-start.2
  129.1 8.7 %copy-start = (f32[8,232,256]{2,1,0:T(8,128)}, f32[8,232,256]{2,1,0:T(8,128)S(1)}, u32[]{:S(2)}) copy-start(f32[8,232,256]{2,1,0:T(8,128)S(1)} %all_to_all.23.got_ref) | copy-start | bytes 5701636
  129.2 15.4 %collective-permute-start.3 = (f32[8,232,256]{2,1,0:T(8,128)S(1)}, f32[8,232,256]{2,1,0:T(8,128)}, u32[]{:S(2)}, u32[]{:S(2)}) collective-permute-start(f32[8,232,256]{2,1,0:T(8,128)S(1)} %all_to_all.23.got_ref), channel_id=1, source_target_pairs={{0,4},{4,0},{8,12},{12,8},{16,20},{20,16},{24,28},{28,24},{32,36},... | collective-permute-start | bytes 5701640 | tf_op jit(solution)/shard_map/ppermute | solution.py:313

commit v3 on v2

v3 whole, which is shorter than its diff:
```python
import functools

import jax
import jax.numpy as jnp
import numpy as np
from jax import lax
from jax.experimental import pallas as pl
from jax.experimental.pallas import tpu as pltpu
from jax.sharding import PartitionSpec as P

LEVEL_SUM = 9
LOW_LEVEL = 6
NY = 8
NZ = 8
MEMBERS = 8
ROWS = 128
BLOCK = 32
SLOTS = 7
EDGE = SLOTS * BLOCK
FLAGS = EDGE + 8
SENT = FLAGS + 8
PART = 64
LANES = 128


def slots_of(levels):
    six, seven, eight = (level in levels for level in (6, 7, 8))
    third = 3 if six else (5 if seven else None)
    fifth = 6 if eight else (5 if six and seven else None)
    return (0, 1, 2, third, 4, fifth, 7)


def place_of(x, y):
    if x % 4 == 0 and y % 4 == 0:
        return (x // 4) * 2 + y // 4
    if x % 4 == 0 and y % 2 == 0:
        return 32 + (x // 4) * 2 + y // 4
    if x % 4 == 2 and y % 4 == 0:
        return 64 + (x // 4) * 2 + y // 4
    if x % 4 == 0:
        return 96 + (x // 4) * 4 + y // 2
    if x % 4 == 2:
        return 160 + (x // 4) * 2 + y // 4
    return 192 + (x // 2) * 2 + y // 4


def hier_line(n):
    h = np.zeros((n, n), np.float32)
    for j in range(n):
        h[j, j] += 1.0
        if j:
            s = j & -j
            h[j, j - s] -= 0.5
            h[j, (j + s) % n] -= 0.5
    return h


def dehier_line(n):
    e = np.zeros((n, n), np.float32)
    e[:, 0] = 1.0
    for k in range(1, n):
        for j in range(n):
            d = min(abs(j - k), n - abs(j - k))
            e[j, k] = max(0.0, 1.0 - d / (k & -k))
    return e


EDGE_ALL = (0, 4, 2, 6, 1, 3, 5, 7)
EDGE_SEVEN = (0, 4, 2, 6)
EDGE_EIGHT = (0, 4)


def one_grid(level, slots):
    n = 1 << (LEVEL_SUM - level)
    span = ROWS // n
    hy, ey = hier_line(n), dehier_line(n)
    forth = np.zeros((SENT, ROWS), np.float32)
    back = np.zeros((ROWS, SENT), np.float32)

    def edge(i, y):
        if i * 64 // span == 63:
            return EDGE + 12 + EDGE_EIGHT.index(y)
        if i * 64 // span == 62:
            return EDGE + 8 + EDGE_SEVEN.index(y)
        return EDGE + EDGE_ALL.index(y)

    for i in range(span):
        for y in range(n):
            up = y * 8 // n
            t = place_of(i * 64 // span, up)
            m = BLOCK * slots.index(t // BLOCK) + t % BLOCK
            s = i & -i
            forth[m, i * n : i * n + n] += hy[y]
            for j in (i - s, i + s) if i else ():
                if j < span:
                    forth[m, j * n : j * n + n] -= 0.5 * hy[y]
            for j in range(span):
                w = max(0.0, 1.0 - abs(j - i) / s) if i else 1.0 - j / span
                back[j * n : j * n + n, m] += w * ey[:, y]
                if i and i + s == span:
                    back[j * n : j * n + n, edge(i, up)] -= 0.5 * w * ey[:, y]
                if i == 0:
                    back[j * n : j * n + n, EDGE + EDGE_ALL.index(up)] += j / span * ey[:, y]
    for y in range(n):
        if level >= 7:
            forth[EDGE + EDGE_SEVEN.index(y * 8 // n), :n] += hy[y]
        if level == 8:
            forth[EDGE + 4 + EDGE_EIGHT.index(y * 8 // n), :n] += hy[y]
    return forth, back


@functools.cache
def row_tables():
    forth, back = [], []
    for own in (6, 7, 8):
        for other in (6, 7, 8):
            slots = slots_of((own, other))
            mine, theirs = one_grid(own, slots), one_grid(other, slots)
            forth.append(np.concatenate([mine[0], theirs[0]], axis=1))
            back.append(mine[1])
    return np.stack(forth), np.stack(back)


def two_part_dot(table, values):
    high = values.astype(jnp.bfloat16)
    low = (values - high.astype(jnp.float32)).astype(jnp.bfloat16)
    dot = functools.partial(jnp.dot, preferred_element_type=jnp.float32)
    return dot(table, high) + dot(table, low)


def number_in(ref, row):
    return jnp.max(ref[row : row + 1, :LANES])


def half_of(ref, core):
    width = ref.shape[1] // 2
    return ref.at[:, pl.ds(pl.multiple_of(core * width, LANES), width)]


def entry_kernel(core_ref, level_ref, coeff_ref, rows_ref, out_ref, sem):
    copy = pltpu.make_async_copy(half_of(rows_ref, 1 - core_ref[0]), out_ref.at[:ROWS], sem)
    copy.start()
    shape = (8, out_ref.shape[1])
    line = lax.broadcasted_iota(jnp.int32, shape, 0)
    out_ref[ROWS:, :] = jnp.where(line == 0, level_ref[0], coeff_ref[0]).astype(jnp.float32)
    copy.wait()


def forth_kernel(core_ref, level_ref, coeff_ref, table_ref, rows_ref, other_ref, out_ref, meta_ref):
    own_level = level_ref[0]
    other_level = number_in(other_ref, ROWS).astype(jnp.int32)
    which = (own_level - LOW_LEVEL) * 3 + other_level - LOW_LEVEL
    chunk = out_ref.shape[2]
    lane = lax.broadcasted_iota(jnp.int32, (1, 2 * ROWS), 1)
    scale = jnp.where(lane < ROWS, coeff_ref[0].astype(jnp.float32), number_in(other_ref, ROWS + 1))
    table = (table_ref[which].astype(jnp.float32) * scale).astype(jnp.bfloat16)
    six = jnp.logical_or(own_level == 6, other_level == 6).astype(jnp.float32)
    eight = jnp.logical_or(own_level == 8, other_level == 8).astype(jnp.float32)
    line = lax.broadcasted_iota(jnp.int32, (SENT - FLAGS, chunk), 0)
    flags = jnp.where(line == 0, six, eight)
    for k in range(MEMBERS):
        start = pl.multiple_of((core_ref[0] * MEMBERS + k) * chunk, LANES)
        own = rows_ref[:, pl.ds(start, chunk)]
        other = other_ref[:ROWS, k * chunk : (k + 1) * chunk]
        values = jnp.concatenate([own, other], axis=0)
        out_ref[k] = two_part_dot(table, values)
        out_ref[k, FLAGS:SENT, :] = flags
    meta_ref[...] = other_ref[ROWS:, :LANES]


def edge_kernel(got_ref, out_ref):
    def total(low, high, held=None):
        total = 0.0
        for k in range(MEMBERS):
            part = got_ref[k, low:high, :]
            total += part if held is None else jnp.where(got_ref[k, held : held + 1, :] == 1.0, part, 0.0)
        return total

    out_ref[0:2, :] = total(0, 8)[0:2]
    out_ref[2:4, :] = total(BLOCK, BLOCK + 8)[0:2]
    out_ref[4:8, :] = total(3 * BLOCK, 3 * BLOCK + 8, FLAGS)[0:4]
    out_ref[8:16, :] = total(EDGE, FLAGS)


def add_kernel(got_ref, out_ref):
    six = [got_ref[k, FLAGS : FLAGS + 1, :] == 1.0 for k in range(MEMBERS)]
    eight = [got_ref[k, FLAGS + 1 : FLAGS + 2, :] == 1.0 for k in range(MEMBERS)]
    slot = lambda k, i: got_ref[k, BLOCK * i : BLOCK * (i + 1), :]
    terms = (
        lambda k: slot(k, 0),
        lambda k: slot(k, 1),
        lambda k: slot(k, 2),
        lambda k: jnp.where(six[k], slot(k, 3), 0.0),
        lambda k: slot(k, 4),
        lambda k: jnp.where(six[k], jnp.where(eight[k], 0.0, slot(k, 5)), slot(k, 3)),
        lambda k: jnp.where(eight[k], slot(k, 5), 0.0),
        lambda k: slot(k, 6),
    )
    for block, term in enumerate(terms):
        total = term(0)
        for k in range(1, MEMBERS):
            total = total + term(k)
        q, low = block // 2, block % 2 * BLOCK
        for j in range(total.shape[1] // LANES):
            out_ref[4 * j + q, low : low + BLOCK, :] = total[:, j * LANES : (j + 1) * LANES]


def total_kernel(got_ref, edge_ref, out_ref):
    total = got_ref[0]
    for k in range(1, MEMBERS):
        total = total + got_ref[k]
    for k in range(MEMBERS):
        out_ref[k, :PART, :] = total
        for j in range(2):
            low = PART + 16 * j
            out_ref[k, low : low + 16, :] = edge_ref[:, j * LANES : (j + 1) * LANES]


def pick_kernel(table_ref, got_ref, out_ref):
    for j in range(2):
        span = slice(j * LANES, (j + 1) * LANES)

        def block(i):
            low = i % 2 * BLOCK
            return table_ref[4 * j + i // 2, low : low + BLOCK, :]

        low = PART + 16 * j
        edge = table_ref[0, low : low + 16, :]
        for k in range(1, MEMBERS):
            edge = edge + table_ref[k, low : low + 16, :]
        for k in range(MEMBERS):
            six = got_ref[k, FLAGS : FLAGS + 1, span] == 1.0
            eight = got_ref[k, FLAGS + 1 : FLAGS + 2, span] == 1.0
            out_ref[k, 0:32, span] = block(0)
            out_ref[k, 32:64, span] = block(1)
            out_ref[k, 64:96, span] = block(2)
            out_ref[k, 96:128, span] = jnp.where(six, block(3), block(5))
            out_ref[k, 128:160, span] = block(4)
            out_ref[k, 160:192, span] = jnp.where(eight, block(6), block(5))
            out_ref[k, 192:224, span] = block(7)
            out_ref[k, EDGE:SENT, span] = edge


def levels_in(level_ref, meta_ref):
    return level_ref[0] - LOW_LEVEL, number_in(meta_ref, 0).astype(jnp.int32) - LOW_LEVEL


def other_back_kernel(level_ref, meta_ref, table_ref, got_ref, out_ref):
    own, other = levels_in(level_ref, meta_ref)
    table = table_ref[other * 3 + own]
    chunk = got_ref.shape[2]
    for k in range(MEMBERS):
        out_ref[:, k * chunk : (k + 1) * chunk] = two_part_dot(table, got_ref[k])


def own_back_kernel(core_ref, level_ref, meta_ref, table_ref, got_ref, out_ref, done_ref, sems):
    own, other = levels_in(level_ref, meta_ref)
    table = table_ref[own * 3 + other]
    chunk = got_ref.shape[2]
    copies = []
    for k in range(MEMBERS):
        done_ref[k] = two_part_dot(table, got_ref[k])
        start = pl.multiple_of((core_ref[0] * MEMBERS + k) * chunk, LANES)
        copy = pltpu.make_async_copy(done_ref.at[k], out_ref.at[:, pl.ds(start, chunk)], sems.at[k])
        copy.start()
        copies.append(copy)
    for copy in copies:
        copy.wait()


def place_kernel(core_ref, values_ref, filled_ref, out_ref, sem):
    copy = pltpu.make_async_copy(values_ref, half_of(out_ref, 1 - core_ref[0]), sem)
    copy.start()
    copy.wait()


def member(y, z, core):
    return (y * NZ + z) * 2 + core


ALONG_Y = [[[member(y, z, core) for y in range(NY)] for z in range(NZ)] for core in (0, 1)]
ALONG_Z = [[[member(y, z, core) for z in range(NZ)] for y in range(NY)] for core in (0, 1)]
FIRST = ALONG_Y[0] + ALONG_Z[1]
SECOND = ALONG_Z[0] + ALONG_Y[1]
VMEM = pl.BlockSpec(memory_space=pltpu.VMEM)
SMEM = pl.BlockSpec(memory_space=pltpu.SMEM)
HBM = pl.BlockSpec(memory_space=pltpu.HBM)
DMA = pltpu.SemaphoreType.DMA


def exchange(values, groups):
    return lax.all_to_all(values, "grp", 0, 0, axis_index_groups=groups, tiled=True)


def f32(*shape):
    return jax.ShapeDtypeStruct(shape, jnp.float32)


def call(kernel, ins, outs, shapes, scratch=(), limit=16, flops=0, moved=0, alias=None):
    return pl.pallas_call(
        kernel,
        in_specs=ins,
        out_specs=outs,
        out_shape=shapes,
        scratch_shapes=scratch,
        compiler_params=pltpu.CompilerParams(vmem_limit_bytes=limit << 20),
        cost_estimate=pl.CostEstimate(flops=flops, bytes_accessed=moved, transcendentals=0),
        input_output_aliases=alias or {},
    )


def shards(grids, first_level, coeffs, slot_map):
    rows = grids[0]
    width = rows.shape[1]
    half = width // 2
    chunk = half // MEMBERS
    slabs = lax.axis_size("slab")
    core = (lax.axis_index("grp") % 2).astype(jnp.int32)[None]
    swap = [(i, i ^ 1) for i in range(lax.axis_size("grp"))]
    to_previous = [(i, (i - 1) % slabs) for i in range(slabs)]
    forth, back = (jnp.asarray(table, jnp.bfloat16) for table in row_tables())

    entry = call(
        entry_kernel, [SMEM, SMEM, SMEM, HBM], VMEM, f32(ROWS + 8, half), (DMA,), limit=60, moved=4 * half * ROWS
    )(core, first_level, coeffs, rows)
    other = lax.ppermute(entry, "grp", swap)
    sent, meta = call(
        forth_kernel, [SMEM, SMEM, SMEM, VMEM, VMEM, VMEM], [VMEM, VMEM],
        [f32(MEMBERS, SENT, chunk), f32(8, LANES)], flops=10**9,
    )(core, first_level, coeffs, forth, rows, other)
    got = exchange(sent, FIRST)

    edge = call(edge_kernel, [VMEM], VMEM, f32(16, chunk), flops=10**6)(got)
    next_edge = lax.ppermute(edge, "slab", to_previous)
    parts = call(add_kernel, [VMEM], VMEM, f32(MEMBERS, PART, LANES), flops=10**8)(got)
    parts = exchange(parts, SECOND)
    total = call(
        total_kernel, [VMEM, VMEM], VMEM, f32(MEMBERS, PART + 32, LANES), flops=10**7
    )(parts, next_edge)
    table = exchange(total, SECOND)
    picked = call(
        pick_kernel, [VMEM, VMEM], VMEM, f32(MEMBERS, SENT, chunk), flops=10**8
    )(table, got)
    final = exchange(picked, FIRST)

    other_out = call(
        other_back_kernel, [SMEM, VMEM, VMEM, VMEM], VMEM, f32(ROWS, half), flops=10**9
    )(first_level, meta, back, final)
    swapped = lax.ppermute(other_out, "grp", swap)
    out = call(
        own_back_kernel, [SMEM, SMEM, VMEM, VMEM, VMEM], HBM, f32(ROWS, width),
        (pltpu.VMEM((MEMBERS, ROWS, chunk), jnp.float32), DMA((MEMBERS,))), flops=10**9,
    )(core, first_level, meta, back, final)
    out = call(
        place_kernel, [SMEM, VMEM, HBM], HBM, f32(ROWS, width), (DMA,), alias={2: 0}
    )(core, swapped, out)
    return out[None]


def solution(mesh):
    in_specs = (P("grp", "slab", None), P("grp"), P("grp"), P("grp", "slab"))
    out_specs = P("grp", "slab", None)
    return jax.shard_map(shards, mesh=mesh, in_specs=in_specs, out_specs=out_specs, check_vma=False)
```

time: 152 us -> 121 us (0.80)
  Pallas kernels: 27.4 us -> 7.01 us
  blocking collectives: 94.4 us -> 75.3 us
  starting transfers between devices: 21.3 us -> 27.7 us
  waiting for transfers between devices: 4.18 us -> 8.35 us
  local copies, waits for them, and re-layouts: 2.57 us -> 0.01 us
    pallas_call x6 -> x9, Pallas kernels: 27.4 us -> 7.01 us  [the longest x1 2.22 us: shards(): call(entry_kernel, [SMEM, SMEM, SMEM, HBM], VMEM, f32(ROWS + 8, half), (D...]
    all_to_all x4 -> x3, blocking collectives: 94.4 us -> 75.3 us  [exchange(): lax.all_to_all(values, 'grp', 0, 0, axis_index_groups=groups, tiled=True)]
    all_to_all x0 -> x1, starting transfers between devices: none -> 6.82 us  [exchange(): lax.all_to_all(values, 'grp', 0, 0, axis_index_groups=groups, tiled=True)]
    all_to_all x0 -> x1, waiting for transfers between devices: none -> 4.06 us  [exchange(): lax.all_to_all(values, 'grp', 0, 0, axis_index_groups=groups, tiled=True)]
    ppermute x4 -> x3, starting transfers between devices: 21.3 us -> 20.8 us  [the longest x1 8.75 us: shards(): other = lax.ppermute(entry, 'grp', swap)]
    ppermute x4 -> x3, waiting for transfers between devices: 4.18 us -> 4.29 us  [the longest x1 2.57 us: shards(): other = lax.ppermute(entry, 'grp', swap)]
  transfers between devices with their start and end apart: 4 -> 4, of which waited for: 1 -> 4; matrix products, arithmetic and copies ran while one was open for 0% -> 0% of each run, Pallas kernels for 4% -> 1%
where the time goes in v3:
time: 121 us; the launch traced here: 120 us
  blocking collectives  75.3 us (62%)
  starting transfers between devices  27.7 us (23%)
  waiting for transfers between devices  8.35 us (7%)
  Pallas kernels  7.01 us (6%)
  between operations  1.72 us (1%)
    all_to_all x3, blocking collectives, exchange(): lax.all_to_all(values, 'grp', 0, 0, axis_index_groups=groups, tiled=True)  75.3 us
    ppermute x1, starting transfers between devices, shards(): other = lax.ppermute(entry, 'grp', swap)  8.75 us
    ppermute x1, starting transfers between devices, shards(): swapped = lax.ppermute(other_out, 'grp', swap)  7.7 us
    all_to_all x1, starting transfers between devices, exchange(): lax.all_to_all(values, 'grp', 0, 0, axis_index_groups=groups, tiled=True)  6.82 us
    ppermute x1, starting transfers between devices, shards(): next_edge = lax.ppermute(edge, 'slab', to_previous)  4.39 us
    all_to_all x1, waiting for transfers between devices, exchange(): lax.all_to_all(values, 'grp', 0, 0, axis_index_groups=groups, tiled=True)  4.06 us
    ppermute x1, waiting for transfers between devices, shards(): other = lax.ppermute(entry, 'grp', swap)  2.57 us
  transfers between devices with their start and end apart: 4, of which 4 were waited for; matrix products, arithmetic and copies ran while one was open for 0% of the time, Pallas kernels for 1%

profile of v3, /device:TPU:1, one launch (start us, length us, event | category | flops | bytes accessed | tf_op | source)
XLA Modules:
  0.0 120.1 jit_solution(6166349804930580931)
XLA Ops:
  0.0 0.0 copy-start.1
  0.0 0.0 copy-start
  1.6 2.2 %shard_map.55 = f32[136,2048]{1,0:T(8,128)} custom-call(s32[1]{0:T(128)} %bitcast.core_ref, s32[1]{0:T(128)S(6)} %copy.8.level_ref, s32[1]{0:T(128)S(6)} %copy.9.coeff_ref, f32[128,4096]{1,0:T(8,128)} %bitcast.3), custom_call_target="tpu_custom_call" | custom-call | bytes 1048576 | tf_op jit(solution)/shard_map/pallas_call | solution.py:323
  3.9 8.7 %collective-permute-start = (f32[136,2048]{1,0:T(8,128)}, f32[136,2048]{1,0:T(8,128)S(1)}, u32[]{:S(2)}, u32[]{:S(2)}) collective-permute-start(f32[136,2048]{1,0:T(8,128)} %shard_map.55), channel_id=1, source_target_pairs={{0,4},{4,0},{8,12},{12,8},{16,20},{20,16},{24,28},{28,24},{32,36},... | collective-permute-start | bytes 3342344 | tf_op jit(solution)/shard_map/ppermute | solution.py:326
  12.6 2.6 %collective-permute-done.other_ref = f32[136,2048]{1,0:T(8,128)S(1)} collective-permute-done((f32[136,2048]{1,0:T(8,128)}, f32[136,2048]{1,0:T(8,128)S(1)}, u32[]{:S(2)}, u32[]{:S(2)}) %collective-permute-start) | collective-permute-done | bytes 1114144 | tf_op jit(solution)/shard_map/ppermute | solution.py:326
  15.2 0.0 copy-done.1
  15.2 0.0 copy-done
  15.2 0.8 shard_map.56
  16.0 32.1 %all_to_all.20.got_ref = f32[8,240,256]{2,1,0:T(8,128)S(1)} all-to-all(f32[8,240,256]{2,1,0:T(8,128)S(1)} %get-tuple-element.8), channel_id=1, replica_groups={{0,64,128,192,256,320,384,448},{8,72,136,200,264,328,392,456},{16,80,14..., dimensions={0} | all-to-all | bytes 3932160 | tf_op jit(solution)/shard_map/all_to_all | solution.py:292
  48.1 0.8 shard_map.57
  48.9 6.8 %all-to-all-start.1 = ((f32[8,64,128]{2,1,0:T(8,128)}), f32[8,64,128]{2,1,0:T(8,128)S(1)}, u32[]{:S(2)}, u32[]{:S(2)}) async-start(f32[8,64,128]{2,1,0:T(8,128)} %shard_map.57), calls=%async_computation.1 | async-start | bytes 524288 | tf_op jit(solution)/shard_map/all_to_all | solution.py:292
  55.8 4.4 %collective-permute-start.1 = (f32[16,256]{1,0:T(8,128)S(1)}, f32[16,256]{1,0:T(8,128)S(1)}, u32[]{:S(2)}, u32[]{:S(2)}) collective-permute-start(f32[16,256]{1,0:T(8,128)S(1)} %shard_map.58), channel_id=1, source_target_pairs={{0,3},{1,0},{2,1},{3,2},{4,7},{5,4},{6,5},{7,6},{8,11},{9,8},{10,9... | collective-permute-start | bytes 49160 | tf_op jit(solution)/shard_map/ppermute | solution.py:334
  60.2 0.8 collective-permute-done.1.edge_ref
  61.0 4.1 %all-to-all-done.1.got_ref = f32[8,64,128]{2,1,0:T(8,128)S(1)} async-done(((f32[8,64,128]{2,1,0:T(8,128)}), f32[8,64,128]{2,1,0:T(8,128)S(1)}, u32[]{:S(2)}, u32[]{:S(2)}) %all-to-all-start.1) | async-done | bytes 262176 | tf_op jit(solution)/shard_map/all_to_all | solution.py:292
  65.1 13.1 %all_to_all.21.table_ref = f32[8,96,128]{2,1,0:T(8,128)S(1)} all-to-all(f32[8,96,128]{2,1,0:T(8,128)S(1)} %shard_map.59), channel_id=1, replica_groups={{0,8,16,24,32,40,48,56},{64,72,80,88,96,104,112,120},{128,136,144,152,1..., dimensions={0} | all-to-all | bytes 786432 | tf_op jit(solution)/shard_map/all_to_all | solution.py:292
  78.2 0.2 shard_map.60
  78.4 0.0 copy-start.2
  78.4 30.1 %all_to_all.22.got_ref = f32[8,240,256]{2,1,0:T(8,128)S(1)} all-to-all(f32[8,240,256]{2,1,0:T(8,128)S(1)} %shard_map.60), channel_id=1, replica_groups={{0,64,128,192,256,320,384,448},{8,72,136,200,264,328,392,456},{16,80,14..., dimensions={0} | all-to-all | bytes 3932160 | tf_op jit(solution)/shard_map/all_to_all | solution.py:292
  108.6 0.0 copy-done.2
  108.6 0.6 shard_map.61
  109.1 7.7 %collective-permute-start.2 = (f32[128,2048]{1,0:T(8,128)S(1)}, f32[128,2048]{1,0:T(8,128)S(1)}, u32[]{:S(2)}, u32[]{:S(2)}) collective-permute-start(f32[128,2048]{1,0:T(8,128)S(1)} %shard_map.61), channel_id=1, source_target_pairs={{0,4},{4,0},{8,12},{12,8},{16,20},{20,16},{24,28},{28,24},{32,36},... | collective-permute-start | bytes 3145736 | tf_op jit(solution)/shard_map/ppermute | solution.py:349
  116.8 1.4 %shard_map.62.filled_ref = f32[128,4096]{1,0:T(8,128)} custom-call(s32[1]{0:T(128)} %bitcast.core_ref, s32[1]{0:T(128)S(6)} %copy.8.level_ref, f32[8,128]{1,0:T(8,128)S(1)} %get-tuple-element.7.meta_ref, bf16[9,128,240]{2,1,0:T(8,128)(2,1)S(1)} %copy-done.2, f32[8,240,256]{2,1,0:T(8,128)S(1)} %all_to_all.22.got_ref), custom_call_target="tpu_custom_call" | custom-call | flops 1000000000 | tf_op jit(solution)/shard_map/pallas_call | solution.py:350
  118.2 0.9 collective-permute-done.2.values_ref
  119.1 1.0 shard_map.63
  (2 shorter events, 0.1 us)
Async XLA Ops:
  0.0 15.2 %copy-start.1 = (bf16[9,240,256]{2,1,0:T(8,128)(2,1)S(1)}, bf16[9,240,256]{2,1,0:T(8,128)(2,1)}, u32[]{:S(2)}) copy-start(bf16[9,240,256]{2,1,0:T(8,128)(2,1)} %constant.23.clone.table_ref) | copy-start | bytes 3317764
  0.0 15.2 %copy-start = (f32[1,128,4096]{2,1,0:T(8,128)S(1)}, f32[1,128,4096]{2,1,0:T(8,128)}, u32[]{:S(2)}) copy-start(f32[1,128,4096]{2,1,0:T(8,128)} %param.6) | copy-start | bytes 6291460
  3.9 11.3 %collective-permute-start = (f32[136,2048]{1,0:T(8,128)}, f32[136,2048]{1,0:T(8,128)S(1)}, u32[]{:S(2)}, u32[]{:S(2)}) collective-permute-start(f32[136,2048]{1,0:T(8,128)} %shard_map.55), channel_id=1, source_target_pairs={{0,4},{4,0},{8,12},{12,8},{16,20},{20,16},{24,28},{28,24},{32,36},... | collective-permute-start | bytes 3342344 | tf_op jit(solution)/shard_map/ppermute | solution.py:326
  48.9 16.2 %all-to-all-start.1 = ((f32[8,64,128]{2,1,0:T(8,128)}), f32[8,64,128]{2,1,0:T(8,128)S(1)}, u32[]{:S(2)}, u32[]{:S(2)}) async-start(f32[8,64,128]{2,1,0:T(8,128)} %shard_map.57), calls=%async_computation.1 | async-start | bytes 524288 | tf_op jit(solution)/shard_map/all_to_all | solution.py:292
  55.8 5.2 %collective-permute-start.1 = (f32[16,256]{1,0:T(8,128)S(1)}, f32[16,256]{1,0:T(8,128)S(1)}, u32[]{:S(2)}, u32[]{:S(2)}) collective-permute-start(f32[16,256]{1,0:T(8,128)S(1)} %shard_map.58), channel_id=1, source_target_pairs={{0,3},{1,0},{2,1},{3,2},{4,7},{5,4},{6,5},{7,6},{8,11},{9,8},{10,9... | collective-permute-start | bytes 49160 | tf_op jit(solution)/shard_map/ppermute | solution.py:334
  78.4 30.2 %copy-start.2 = (bf16[9,128,240]{2,1,0:T(8,128)(2,1)S(1)}, bf16[9,128,240]{2,1,0:T(8,128)(2,1)}, u32[]{:S(2)}) copy-start(bf16[9,128,240]{2,1,0:T(8,128)(2,1)} %constant.24.clone.table_ref) | copy-start | bytes 1658884
  109.1 10.0 %collective-permute-start.2 = (f32[128,2048]{1,0:T(8,128)S(1)}, f32[128,2048]{1,0:T(8,128)S(1)}, u32[]{:S(2)}, u32[]{:S(2)}) collective-permute-start(f32[128,2048]{1,0:T(8,128)S(1)} %shard_map.61), channel_id=1, source_target_pairs={{0,4},{4,0},{8,12},{12,8},{16,20},{20,16},{24,28},{28,24},{32,36},... | collective-permute-start | bytes 3145736 | tf_op jit(solution)/shard_map/ppermute | solution.py:349

commit v4 on v3

v4 whole, which is shorter than its diff:
```python
import functools

import jax
import jax.numpy as jnp
import numpy as np
from jax import lax
from jax.experimental import pallas as pl
from jax.experimental.pallas import tpu as pltpu
from jax.sharding import PartitionSpec as P

LEVEL_SUM = 9
LOW_LEVEL = 6
NY = 8
NZ = 8
MEMBERS = 4
ROWS = 128
PLANE = 8
BLOCK = 32
SLOTS = 7
THERE = SLOTS * BLOCK
FLAGS = THERE + PLANE
SENT = FLAGS + 8
ENTRY = 2 * (ROWS + PLANE)
TABLE = 8 * BLOCK + PLANE
LANES = 128
BLOCKS_OF = {6: (0, 1, 3, 4), 7: (0, 1, 2, 5), 8: (0, 2, 6, 7)}


def slots_of(levels):
    six, seven, eight = (level in levels for level in (6, 7, 8))
    third = 3 if six else (5 if seven else None)
    fifth = 6 if eight else (5 if six and seven else None)
    return (0, 1, 2, third, 4, fifth, 7)


def place_of(x, y):
    if x % 4 == 0 and y % 4 == 0:
        return (x // 4) * 2 + y // 4
    if x % 4 == 0 and y % 2 == 0:
        return 32 + (x // 4) * 2 + y // 4
    if x % 4 == 2 and y % 4 == 0:
        return 64 + (x // 4) * 2 + y // 4
    if x % 4 == 0:
        return 96 + (x // 4) * 4 + y // 2
    if x % 4 == 2:
        return 160 + (x // 4) * 2 + y // 4
    return 192 + (x // 2) * 2 + y // 4


def hier_line(n):
    h = np.zeros((n, n), np.float32)
    for j in range(n):
        h[j, j] += 1.0
        if j:
            s = j & -j
            h[j, j - s] -= 0.5
            h[j, (j + s) % n] -= 0.5
    return h


def dehier_line(n):
    e = np.zeros((n, n), np.float32)
    e[:, 0] = 1.0
    for k in range(1, n):
        for j in range(n):
            d = min(abs(j - k), n - abs(j - k))
            e[j, k] = max(0.0, 1.0 - d / (k & -k))
    return e


def one_grid(level, slots):
    n = 1 << (LEVEL_SUM - level)
    span = ROWS // n
    hy, ey = hier_line(n), dehier_line(n)
    forth = np.zeros((SENT, ROWS + PLANE), np.float32)
    back = np.zeros((ROWS, FLAGS), np.float32)
    for i in range(span):
        for y in range(n):
            t = place_of(i * 64 // span, y * 8 // n)
            m = BLOCK * slots.index(t // BLOCK) + t % BLOCK
            s = i & -i
            steps = [(i, 1.0)] + ([(i - s, -0.5), (i + s, -0.5)] if i else [])
            for j, w in steps:
                forth[m, j * n : j * n + n] += w * hy[y]
            for j in range(span):
                w = max(0.0, 1.0 - abs(j - i) / s) if i else 1.0 - j / span
                back[j * n : j * n + n, m] += w * ey[:, y]
    for y in range(n):
        t = THERE + y * 8 // n
        forth[t, ROWS : ROWS + n] += hy[y]
        for j in range(span):
            back[j * n : j * n + n, t] += j / span * ey[:, y]
    return forth, back


@functools.cache
def row_tables():
    forth, back = [], []
    for own in (6, 7, 8):
        for other in (6, 7, 8):
            slots = slots_of((own, other))
            mine, theirs = one_grid(own, slots), one_grid(other, slots)
            forth.append(np.concatenate([mine[0], theirs[0]], axis=1))
            back.append(mine[1])
    return np.stack(forth), np.stack(back)


def two_part_dot(table, values):
    high = values.astype(jnp.bfloat16)
    low = (values - high.astype(jnp.float32)).astype(jnp.bfloat16)
    dot = functools.partial(jnp.dot, preferred_element_type=jnp.float32)
    return dot(table, high) + dot(table, low)


def number_in(ref, row):
    return jnp.max(ref[row : row + 1, :LANES])


def core_here():
    return lax.axis_index("grp") % 2


def half_of(ref, core, rows=slice(None)):
    width = ref.shape[1] // 2
    return ref.at[rows, pl.ds(pl.multiple_of(core * width, LANES), width)]


def entry_kernel(level_ref, coeff_ref, rows_ref, out_ref, own_ref, other_ref):
    core = core_here()
    half = out_ref.shape[1]
    mine = pl.ds(pl.multiple_of(core * half, LANES), half)
    theirs = pl.ds(pl.multiple_of((1 - core) * half, LANES), half)
    own_ref[...] = rows_ref[:PLANE, mine]
    other_ref[...] = rows_ref[:PLANE, theirs]
    out_ref[:ROWS, :] = rows_ref[:, theirs]
    line = lax.broadcasted_iota(jnp.int32, (8, half), 0)
    out_ref[ROWS:, :] = jnp.where(line == 0, level_ref[0], coeff_ref[0]).astype(jnp.float32)


def forth_kernel(level_ref, coeff_ref, table_ref, rows_ref, own_next_ref, other_ref, other_next_ref, out_ref, meta_ref):
    own_level = level_ref[0]
    other_level = number_in(other_ref, ROWS).astype(jnp.int32)
    which = (own_level - LOW_LEVEL) * 3 + other_level - LOW_LEVEL
    chunk = out_ref.shape[2]
    lane = lax.broadcasted_iota(jnp.int32, (1, ENTRY), 1)
    scale = jnp.where(lane < ENTRY // 2, coeff_ref[0].astype(jnp.float32), number_in(other_ref, ROWS + 1))
    table = (table_ref[which].astype(jnp.float32) * scale).astype(jnp.bfloat16)
    six = jnp.logical_or(own_level == 6, other_level == 6).astype(jnp.float32)
    eight = jnp.logical_or(own_level == 8, other_level == 8).astype(jnp.float32)
    width = chunk // 2
    line = lax.broadcasted_iota(jnp.int32, (SENT - FLAGS, width), 0)
    flags = jnp.where(line == 0, six, eight)
    first = core_here() * MEMBERS * chunk
    for k in range(MEMBERS):
        for h in range(2):
            here = slice(h * width, (h + 1) * width)
            low = k * chunk + h * width
            span = slice(low, low + width)
            own = rows_ref[:, pl.ds(pl.multiple_of(first + low, LANES), width)]
            values = jnp.concatenate(
                [own, own_next_ref[:, span], other_ref[:ROWS, span], other_next_ref[:, span]], axis=0
            )
            out_ref[k, :, here] = two_part_dot(table, values)
            out_ref[k, FLAGS:SENT, here] = flags
    meta_ref[...] = other_ref[ROWS:, :LANES]


def add_kernel(got_ref, out_ref):
    for j in range(MEMBERS):
        lanes = slice(j * LANES, (j + 1) * LANES)
        six = [got_ref[k, FLAGS : FLAGS + 1, lanes] == 1.0 for k in range(MEMBERS)]
        eight = [got_ref[k, FLAGS + 1 : FLAGS + 2, lanes] == 1.0 for k in range(MEMBERS)]
        slot = lambda k, i: got_ref[k, BLOCK * i : BLOCK * (i + 1), lanes]
        terms = (
            lambda k: slot(k, 0),
            lambda k: slot(k, 1),
            lambda k: slot(k, 2),
            lambda k: jnp.where(six[k], slot(k, 3), 0.0),
            lambda k: slot(k, 4),
            lambda k: jnp.where(six[k], jnp.where(eight[k], 0.0, slot(k, 5)), slot(k, 3)),
            lambda k: jnp.where(eight[k], slot(k, 5), 0.0),
            lambda k: slot(k, 6),
            lambda k: got_ref[k, THERE:FLAGS, lanes],
        )
        for block, term in enumerate(terms):
            total = term(0)
            for k in range(1, MEMBERS):
                total = total + term(k)
            out_ref[j, BLOCK * block : BLOCK * block + total.shape[0], :] = total


def total_kernel(got_ref, out_ref):
    total = got_ref[0]
    for k in range(1, MEMBERS):
        total = total + got_ref[k]
    for k in range(MEMBERS):
        out_ref[k] = total


def pick_kernel(table_ref, got_ref, out_ref):
    for j in range(MEMBERS):
        lanes = slice(j * LANES, (j + 1) * LANES)
        block = lambda i: table_ref[j, BLOCK * i : BLOCK * (i + 1), :]
        for k in range(MEMBERS):
            six = got_ref[k, FLAGS : FLAGS + 1, lanes] == 1.0
            eight = got_ref[k, FLAGS + 1 : FLAGS + 2, lanes] == 1.0
            out_ref[k, 0:32, lanes] = block(0)
            out_ref[k, 32:64, lanes] = block(1)
            out_ref[k, 64:96, lanes] = block(2)
            out_ref[k, 96:128, lanes] = jnp.where(six, block(3), block(5))
            out_ref[k, 128:160, lanes] = block(4)
            out_ref[k, 160:192, lanes] = jnp.where(eight, block(6), block(5))
            out_ref[k, 192:224, lanes] = block(7)
            out_ref[k, THERE:FLAGS, lanes] = table_ref[j, 8 * BLOCK : TABLE, :]


def levels_in(level_ref, meta_ref):
    return level_ref[0] - LOW_LEVEL, number_in(meta_ref, 0).astype(jnp.int32) - LOW_LEVEL


def pieces(ref):
    width = ref.shape[2] // 2
    for k in range(MEMBERS):
        for h in range(2):
            yield ref[k, :, h * width : (h + 1) * width]


def other_back_kernel(level_ref, meta_ref, table_ref, got_ref, out_ref):
    own, other = levels_in(level_ref, meta_ref)
    table = table_ref[other * 3 + own]
    for i, values in enumerate(pieces(got_ref)):
        width = values.shape[1]
        out_ref[:, i * width : (i + 1) * width] = two_part_dot(table, values)


def own_back_kernel(level_ref, meta_ref, table_ref, got_ref, out_ref, done_ref, sems):
    own, other = levels_in(level_ref, meta_ref)
    table = table_ref[own * 3 + other]
    first = core_here() * 2 * MEMBERS
    copies = []
    for i, values in enumerate(pieces(got_ref)):
        width = values.shape[1]
        done_ref[i] = two_part_dot(table, values)
        start = pl.multiple_of((first + i) * width, LANES)
        copy = pltpu.make_async_copy(done_ref.at[i], out_ref.at[:, pl.ds(start, width)], sems.at[i])
        copy.start()
        copies.append(copy)
    for copy in copies:
        copy.wait()


def place_kernel(values_ref, filled_ref, out_ref, sem):
    copy = pltpu.make_async_copy(values_ref, half_of(out_ref, 1 - core_here()), sem)
    copy.start()
    copy.wait()


def member(y, z, core):
    return (y % NY * NZ + z % NZ) * 2 + core


TILES = [
    [member(2 * a + i + core, 2 * b + j + core, core) for i in (0, 1) for j in (0, 1)]
    for core in (0, 1)
    for a in range(NY // 2)
    for b in range(NZ // 2)
]
ALONG_Y = [[[member(2 * a + i, z, core) for a in range(NY // 2)] for i in (0, 1) for z in range(NZ)] for core in (0, 1)]
ALONG_Z = [[[member(y, 2 * b + j, core) for b in range(NZ // 2)] for j in (0, 1) for y in range(NY)] for core in (0, 1)]
LINES = ALONG_Y[0] + ALONG_Z[1]
OTHER_LINES = ALONG_Z[0] + ALONG_Y[1]
VMEM = pl.BlockSpec(memory_space=pltpu.VMEM)
SMEM = pl.BlockSpec(memory_space=pltpu.SMEM)
HBM = pl.BlockSpec(memory_space=pltpu.HBM)
DMA = pltpu.SemaphoreType.DMA


def exchange(values, groups):
    return lax.all_to_all(values, "grp", 0, 0, axis_index_groups=groups, tiled=True)


def f32(*shape):
    return jax.ShapeDtypeStruct(shape, jnp.float32)


def call(kernel, name, ins, outs, shapes, scratch=(), limit=16, flops=0, moved=0, alias=None):
    return pl.pallas_call(
        kernel,
        in_specs=ins,
        out_specs=outs,
        out_shape=shapes,
        scratch_shapes=scratch,
        compiler_params=pltpu.CompilerParams(vmem_limit_bytes=limit << 20),
        cost_estimate=pl.CostEstimate(flops=flops, bytes_accessed=moved, transcendentals=0),
        input_output_aliases=alias or {},
        name=name,
    )


def shards(grids, first_level, coeffs, slot_map):
    rows = grids[0]
    width = rows.shape[1]
    half = width // 2
    chunk = half // MEMBERS
    slabs = lax.axis_size("slab")
    members = lax.axis_size("grp")
    swap = [(i, i ^ 1) for i in range(members)]
    forth, back = (jnp.asarray(table, jnp.bfloat16) for table in row_tables())

    def to_previous(values, turn):
        pairs = [
            (g * slabs + s, (g ^ turn) * slabs + (s - 1) % slabs)
            for g in range(members)
            for s in range(slabs)
        ]
        return lax.ppermute(values, ("grp", "slab"), pairs)

    entry, own_plane, other_plane = call(
        entry_kernel, "entry", [SMEM, SMEM, VMEM], [VMEM] * 3,
        [f32(ROWS + 8, half), f32(PLANE, half), f32(PLANE, half)],
    )(first_level, coeffs, rows)
    other_next = to_previous(other_plane, 1)
    own_next = to_previous(own_plane, 0)
    other = lax.ppermute(entry, "grp", swap)
    sent, meta = call(
        forth_kernel, "forth", [SMEM, SMEM] + [VMEM] * 5, [VMEM, VMEM],
        [f32(MEMBERS, SENT, chunk), f32(8, LANES)], flops=10**9,
    )(first_level, coeffs, forth, rows, own_next, other, other_next)
    got = exchange(sent, TILES)

    parts = call(add_kernel, "add", [VMEM], VMEM, f32(MEMBERS, TABLE, LANES), flops=10**8)(got)
    for groups in (LINES, OTHER_LINES):
        parts = exchange(parts, groups)
        parts = call(total_kernel, "total", [VMEM], VMEM, f32(MEMBERS, TABLE, LANES), flops=10**8)(parts)
    table = exchange(parts, LINES)
    picked = call(
        pick_kernel, "pick", [VMEM, VMEM], VMEM, f32(MEMBERS, FLAGS, chunk), flops=10**8
    )(table, got)
    final = exchange(picked, TILES)

    other_out = call(
        other_back_kernel, "other_back", [SMEM, VMEM, VMEM, VMEM], VMEM, f32(ROWS, half), flops=10**9
    )(first_level, meta, back, final)
    swapped = lax.ppermute(other_out, "grp", swap)
    out = call(
        own_back_kernel, "own_back", [SMEM, VMEM, VMEM, VMEM], HBM, f32(ROWS, width),
        (pltpu.VMEM((2 * MEMBERS, ROWS, chunk // 2), jnp.float32), DMA((2 * MEMBERS,))), flops=10**9,
    )(first_level, meta, back, final)
    out = call(
        place_kernel, "place", [VMEM, HBM], HBM, f32(ROWS, width), (DMA,), alias={1: 0}
    )(swapped, out)
    return out[None]


def solution(mesh):
    in_specs = (P("grp", "slab", None), P("grp"), P("grp"), P("grp", "slab"))
    out_specs = P("grp", "slab", None)
    return jax.shard_map(shards, mesh=mesh, in_specs=in_specs, out_specs=out_specs, check_vma=False)
```

time: 121 us -> 118 us (0.975)
  blocking collectives: 75.3 us -> 86.9 us
  starting transfers between devices: 27.7 us -> 18.6 us
  waiting for transfers between devices: 8.35 us -> 4.65 us
  Pallas kernels: 7.01 us -> 4.78 us
  local copies, waits for them, and re-layouts: 0.01 us -> 1.59 us
    all_to_all x3 -> x5, blocking collectives: 75.3 us -> 86.9 us  [exchange(): lax.all_to_all(values, 'grp', 0, 0, axis_index_groups=groups, tiled=True)]
    all_to_all x1 -> x0, starting transfers between devices: 6.82 us -> none  [exchange(): lax.all_to_all(values, 'grp', 0, 0, axis_index_groups=groups, tiled=True)]
    all_to_all x1 -> x0, waiting for transfers between devices: 4.06 us -> none  [exchange(): lax.all_to_all(values, 'grp', 0, 0, axis_index_groups=groups, tiled=True)]
    ppermute x1 -> x2, waiting for transfers between devices: 0.85 us -> 3.78 us  [to_previous(): return lax.ppermute(values, ('grp', 'slab'), pairs)]
    ppermute x1, waiting for transfers between devices: 2.57 us -> 0.01 us  [shards(): other = lax.ppermute(entry, 'grp', swap)]
    pallas_call x9, Pallas kernels: 7.01 us -> 4.78 us  [the longest x1 1.39 us: shards(): call(own_back_kernel, 'own_back', [SMEM, VMEM, VMEM, VMEM], HBM, f32(ROWS...]
    ppermute x1, starting transfers between devices: 7.7 us -> 5.84 us  [shards(): swapped = lax.ppermute(other_out, 'grp', swap)]
    unnamed x6, local copies, waits for them, and re-layouts: 0.01 us -> 1.59 us
  transfers between devices with their start and end apart: 4 -> 4, of which waited for: 4 -> 3; matrix products, arithmetic and copies ran while one was open for 0% -> 0% of each run, Pallas kernels for 1% -> 1%
where the time goes in v4:
time: 118 us
  blocking collectives  86.9 us (74%)
  starting transfers between devices  18.6 us (16%)
  Pallas kernels  4.78 us (4%)
  waiting for transfers between devices  4.65 us (4%)
  local copies, waits for them, and re-layouts  1.59 us (1%)
  between operations  1.4 us (1%)
    all_to_all x5, blocking collectives, exchange(): lax.all_to_all(values, 'grp', 0, 0, axis_index_groups=groups, tiled=True)  86.9 us
    ppermute x1, starting transfers between devices, shards(): other = lax.ppermute(entry, 'grp', swap)  8.88 us
    ppermute x1, starting transfers between devices, shards(): swapped = lax.ppermute(other_out, 'grp', swap)  5.84 us
    ppermute x2, starting transfers between devices, to_previous(): return lax.ppermute(values, ('grp', 'slab'), pairs)  3.84 us
    ppermute x2, waiting for transfers between devices, to_previous(): return lax.ppermute(values, ('grp', 'slab'), pairs)  3.78 us
  transfers between devices with their start and end apart: 4, of which 3 were waited for; matrix products, arithmetic and copies ran while one was open for 0% of the time, Pallas kernels for 1%

profile of v4, /device:TPU:1, one launch (start us, length us, event | category | flops | bytes accessed | tf_op | source)
XLA Modules:
  0.0 117.9 jit_solution(15712117051936623067)
XLA Ops:
  1.3 0.0 copy-start
  1.3 1.6 %copy-done = f32[1,128,4096]{2,1,0:T(8,128)S(1)} copy-done((f32[1,128,4096]{2,1,0:T(8,128)S(1)}, f32[1,128,4096]{2,1,0:T(8,128)}, u32[]{:S(2)}) %copy-start) | copy-done | bytes 2097176
  2.9 0.1 entry.1
  3.0 8.9 %collective-permute-start.1 = (f32[136,2048]{1,0:T(8,128)S(1)}, f32[136,2048]{1,0:T(8,128)S(1)}, u32[]{:S(2)}, u32[]{:S(2)}) collective-permute-start(f32[136,2048]{1,0:T(8,128)S(1)} %get-tuple-element.11), channel_id=1, source_target_pairs={{0,4},{4,0},{8,12},{12,8},{16,20},{20,16},{24,28},{28,24},{32,36},... | collective-permute-start | bytes 3342344 | tf_op jit(solution)/shard_map/ppermute | solution.py:324
  11.9 1.9 %collective-permute-start = (f32[8,2048]{1,0:T(8,128)S(1)}, f32[8,2048]{1,0:T(8,128)S(1)}, u32[]{:S(2)}, u32[]{:S(2)}) collective-permute-start(f32[8,2048]{1,0:T(8,128)S(1)} %get-tuple-element.10), channel_id=1, source_target_pairs={{0,3},{1,0},{2,1},{3,2},{4,7},{5,4},{6,5},{7,6},{8,11},{9,8},{10,9... | collective-permute-start | bytes 196616 | tf_op jit(solution)/shard_map/ppermute | solution.py:316
  13.8 1.9 %collective-permute-start.2 = (f32[8,2048]{1,0:T(8,128)S(1)}, f32[8,2048]{1,0:T(8,128)S(1)}, u32[]{:S(2)}, u32[]{:S(2)}) collective-permute-start(f32[8,2048]{1,0:T(8,128)S(1)} %get-tuple-element.12), channel_id=1, source_target_pairs={{0,7},{1,4},{2,5},{3,6},{4,3},{5,0},{6,1},{7,2},{8,15},{9,12},{10,... | collective-permute-start | bytes 196616 | tf_op jit(solution)/shard_map/ppermute | solution.py:316
  15.7 1.7 %collective-permute-done.own_next_ref = f32[8,2048]{1,0:T(8,128)S(1)} collective-permute-done((f32[8,2048]{1,0:T(8,128)S(1)}, f32[8,2048]{1,0:T(8,128)S(1)}, u32[]{:S(2)}, u32[]{:S(2)}) %collective-permute-start) | collective-permute-done | bytes 65568 | tf_op jit(solution)/shard_map/ppermute | solution.py:316
  17.4 2.1 %collective-permute-done.2.other_next_ref = f32[8,2048]{1,0:T(8,128)S(1)} collective-permute-done((f32[8,2048]{1,0:T(8,128)S(1)}, f32[8,2048]{1,0:T(8,128)S(1)}, u32[]{:S(2)}, u32[]{:S(2)}) %collective-permute-start.2) | collective-permute-done | bytes 65568 | tf_op jit(solution)/shard_map/ppermute | solution.py:316
  19.5 0.0 collective-permute-done.1.other_ref
  19.5 0.0 copy-done.1
  19.5 1.3 %forth.1 = (f32[4,240,512]{2,1,0:T(8,128)S(1)}, f32[8,128]{1,0:T(8,128)S(1)}) custom-call(s32[1]{0:T(128)S(6)} %copy.8.level_ref, s32[1]{0:T(128)S(6)} %copy.9.coeff_ref, bf16[9,240,272]{2,1,0:T(8,128)(2,1)S(1)} %copy-done.1, f32[128,4096]{1,0:T(8,128)S(1)} %bitcast.3, f32[8,2048]{1,0:T(8,128)S(1)} %collective-permute-done.own_next_ref, ...), custom_call_target="tpu_custom_call" | custom-call | flops 1000000000 | tf_op jit(solution)/shard_map/forth/pallas_call | solution.py:325
  20.8 23.4 %all_to_all.25.got_ref = f32[4,240,512]{2,1,0:T(8,128)S(1)} all-to-all(f32[4,240,512]{2,1,0:T(8,128)S(1)} %get-tuple-element.14), channel_id=1, replica_groups={{0,8,64,72},{16,24,80,88},{32,40,96,104},{48,56,112,120},{128,136,192,2..., dimensions={0} | all-to-all | bytes 3932160 | tf_op jit(solution)/shard_map/all_to_all | solution.py:279
  44.2 0.2 add.1
  44.4 14.6 %all_to_all.26.got_ref = f32[4,264,128]{2,1,0:T(8,128)S(1)} all-to-all(f32[4,264,128]{2,1,0:T(8,128)S(1)} %add.1), channel_id=1, replica_groups={{0,128,256,384},{8,136,264,392},{16,144,272,400},{24,152,280,408},{32,1..., dimensions={0} | all-to-all | bytes 1081344 | tf_op jit(solution)/shard_map/all_to_all | solution.py:279
  59.1 17.1 %all_to_all.27.got_ref = f32[4,264,128]{2,1,0:T(8,128)S(1)} all-to-all(f32[4,264,128]{2,1,0:T(8,128)S(1)} %total.2), channel_id=1, replica_groups={{0,16,32,48},{64,80,96,112},{128,144,160,176},{192,208,224,240},{256,27..., dimensions={0} | all-to-all | bytes 1081344 | tf_op jit(solution)/shard_map/all_to_all | solution.py:279
  76.2 14.1 %all_to_all.28.table_ref = f32[4,264,128]{2,1,0:T(8,128)S(1)} all-to-all(f32[4,264,128]{2,1,0:T(8,128)S(1)} %total.3), channel_id=1, replica_groups={{0,128,256,384},{8,136,264,392},{16,144,272,400},{24,152,280,408},{32,1..., dimensions={0} | all-to-all | bytes 1081344 | tf_op jit(solution)/shard_map/all_to_all | solution.py:279
  90.3 0.2 pick.1
  90.5 0.0 copy-start.2
  90.5 17.7 %all_to_all.29.got_ref = f32[4,232,512]{2,1,0:T(8,128)S(1)} all-to-all(f32[4,232,512]{2,1,0:T(8,128)S(1)} %pick.1), channel_id=1, replica_groups={{0,8,64,72},{16,24,80,88},{32,40,96,104},{48,56,112,120},{128,136,192,2..., dimensions={0} | all-to-all | bytes 3801088 | tf_op jit(solution)/shard_map/all_to_all | solution.py:279
  108.3 0.6 other_back.1
  108.8 5.8 %collective-permute-start.3 = (f32[128,2048]{1,0:T(8,128)S(1)}, f32[128,2048]{1,0:T(8,128)S(1)}, u32[]{:S(2)}, u32[]{:S(2)}) collective-permute-start(f32[128,2048]{1,0:T(8,128)S(1)} %other_back.1), channel_id=1, source_target_pairs={{0,4},{4,0},{8,12},{12,8},{16,20},{20,16},{24,28},{28,24},{32,36},... | collective-permute-start | bytes 3145736 | tf_op jit(solution)/shard_map/ppermute | solution.py:344
  114.7 1.4 %own_back.1.filled_ref = f32[128,4096]{1,0:T(8,128)} custom-call(s32[1]{0:T(128)S(6)} %copy.8.level_ref, f32[8,128]{1,0:T(8,128)S(1)} %get-tuple-element.13.meta_ref, bf16[9,128,232]{2,1,0:T(8,128)(2,1)S(1)} %copy-done.2, f32[4,232,512]{2,1,0:T(8,128)S(1)} %all_to_all.29.got_ref), custom_call_target="tpu_custom_call" | custom-call | flops 1000000000 | tf_op jit(solution)/shard_map/own_back/pallas_call | solution.py:345
  116.1 0.9 collective-permute-done.3.values_ref
  116.9 1.0 place.1
  (4 shorter events, 0.1 us)
Async XLA Ops:
  1.3 1.6 %copy-start = (f32[1,128,4096]{2,1,0:T(8,128)S(1)}, f32[1,128,4096]{2,1,0:T(8,128)}, u32[]{:S(2)}) copy-start(f32[1,128,4096]{2,1,0:T(8,128)} %param.6) | copy-start | bytes 6291460
  2.9 16.6 %copy-start.1 = (bf16[9,240,272]{2,1,0:T(8,128)(2,1)S(1)}, bf16[9,240,272]{2,1,0:T(8,128)(2,1)}, u32[]{:S(2)}) copy-start(bf16[9,240,272]{2,1,0:T(8,128)(2,1)} %constant.4.clone.table_ref) | copy-start | bytes 3525124
  3.0 16.5 %collective-permute-start.1 = (f32[136,2048]{1,0:T(8,128)S(1)}, f32[136,2048]{1,0:T(8,128)S(1)}, u32[]{:S(2)}, u32[]{:S(2)}) collective-permute-start(f32[136,2048]{1,0:T(8,128)S(1)} %get-tuple-element.11), channel_id=1, source_target_pairs={{0,4},{4,0},{8,12},{12,8},{16,20},{20,16},{24,28},{28,24},{32,36},... | collective-permute-start | bytes 3342344 | tf_op jit(solution)/shard_map/ppermute | solution.py:324
  11.9 5.5 %collective-permute-start = (f32[8,2048]{1,0:T(8,128)S(1)}, f32[8,2048]{1,0:T(8,128)S(1)}, u32[]{:S(2)}, u32[]{:S(2)}) collective-permute-start(f32[8,2048]{1,0:T(8,128)S(1)} %get-tuple-element.10), channel_id=1, source_target_pairs={{0,3},{1,0},{2,1},{3,2},{4,7},{5,4},{6,5},{7,6},{8,11},{9,8},{10,9... | collective-permute-start | bytes 196616 | tf_op jit(solution)/shard_map/ppermute | solution.py:316
  13.8 5.7 %collective-permute-start.2 = (f32[8,2048]{1,0:T(8,128)S(1)}, f32[8,2048]{1,0:T(8,128)S(1)}, u32[]{:S(2)}, u32[]{:S(2)}) collective-permute-start(f32[8,2048]{1,0:T(8,128)S(1)} %get-tuple-element.12), channel_id=1, source_target_pairs={{0,7},{1,4},{2,5},{3,6},{4,3},{5,0},{6,1},{7,2},{8,15},{9,12},{10,... | collective-permute-start | bytes 196616 | tf_op jit(solution)/shard_map/ppermute | solution.py:316
  90.5 17.8 %copy-start.2 = (bf16[9,128,232]{2,1,0:T(8,128)(2,1)S(1)}, bf16[9,128,232]{2,1,0:T(8,128)(2,1)}, u32[]{:S(2)}) copy-start(bf16[9,128,232]{2,1,0:T(8,128)(2,1)} %constant.5.clone.table_ref) | copy-start | bytes 1603588
  108.8 8.1 %collective-permute-start.3 = (f32[128,2048]{1,0:T(8,128)S(1)}, f32[128,2048]{1,0:T(8,128)S(1)}, u32[]{:S(2)}, u32[]{:S(2)}) collective-permute-start(f32[128,2048]{1,0:T(8,128)S(1)} %other_back.1), channel_id=1, source_target_pairs={{0,4},{4,0},{8,12},{12,8},{16,20},{20,16},{24,28},{28,24},{32,36},... | collective-permute-start | bytes 3145736 | tf_op jit(solution)/shard_map/ppermute | solution.py:344
